TPU v7x, 32 devices: a whole 2x2x4 slice. The times are simulated.
32 devices in a mesh: grp: 2 (over y), gx: 4 (over z), gy: 2 (over x), gz: 2 (over core).
Axes of the slice: x: 2, y: 2, z: 4, core: 2. Of those that a mesh axis runs over, the one named last changes fastest.
Arguments:
- position: float32 [64, 16, 4, 256], P(None, ('grp', 'gx'), 'gy', 'gz'), parts along dimension 1, may hold values from -6 to 6
- momentum: float32 [64, 16, 4, 256], P(None, ('grp', 'gx'), 'gy', 'gz'), parts along dimension 1, may hold values from -6 to 6
- noise: bfloat16 [3, 64, 16, 4, 256], P(None, None, ('grp', 'gx'), 'gy', 'gz'), parts along dimension 2, may hold values from -6 to 6
- filter_in: bfloat16 [64, 64, 3, 3, 3], P('gx', 'gy'), may hold values from -0.15625 to 0.15625
- filter_out: bfloat16 [64, 64, 3, 3, 3], P('gx', 'gy'), may hold values from -0.15625 to 0.15625
- bias: float32 [64], replicated, may hold values from -4 to 4
Outputs:
- final_position: float32 [64, 16, 4, 256], P(None, ('grp', 'gx'), 'gy', 'gz'), parts along dimension 1
- final_momentum: float32 [64, 16, 4, 256], P(None, ('grp', 'gx'), 'gy', 'gz'), parts along dimension 1
There are 2 independent parts, one for each index of `grp`. A program takes and returns all parts, laid end to end along the dimension named above; an argument that names none is the same for every part. Nothing has to cross between parts.
All inputs are finite; a program needn't handle non-finite values.
Results may differ from a plain program's by a relative error of at most 0.0013.
Values may be sent and summed in bfloat16 or wider, within the bound.
A program may use at most 64 MiB of HBM per device.

v0:
```python
import functools

import jax
import jax.numpy as jnp
from jax import lax
from jax.experimental import pallas as pl
from jax.experimental.pallas import tpu as pltpu
from jax.sharding import PartitionSpec as P

EDGE = 16
MESH = pl.DeviceIdType.MESH


def kernel(steps, sizes, pos_ref, mom_ref, noise_ref, w_ref, bias_ref,
           q_out, p_out, a1, a2, b1, b2, eq, eh, t_ref, q_ref, p_ref, send, recv, *gather):
    nx, ny, nz = sizes
    c = pos_ref.shape[0]
    inside = len(gather) > 0
    if inside:
        wg, wf, wsend, wrecv = gather
    x, z, lanes = q_ref.shape
    y = lanes // c
    full = eq.shape[1]
    wrap = ny == 2
    slots = eq.shape[2] // c
    own = slice(EDGE, EDGE + z)
    mine = slice(lanes, 2 * lanes)

    ix, iy, iz = lax.axis_index("gx"), lax.axis_index("gy"), lax.axis_index("gz")
    up = {"gx": lax.rem(ix + 1, nx), "gy": lax.rem(iy + 1, ny), "gz": lax.rem(iz + 1, nz)}
    down = {
        "gx": lax.rem(ix + nx - 1, nx),
        "gy": lax.rem(iy + ny - 1, ny),
        "gz": lax.rem(iz + nz - 1, nz),
    }

    def at_side(**which):
        return {axis: which[axis][axis] for axis in which}

    def early(buf):
        core = slice(2, 2 + x)
        low, high = slice(0, EDGE), slice(z + EDGE, full)
        block = buf.at[core, own, mine]
        edges = (
            (up, buf.at[core, z : z + EDGE, mine], low),
            (down, buf.at[core, EDGE : 2 * EDGE, mine], high),
        )
        out = []
        for side, source, rows in edges:
            out.append((at_side(gz=side), source, buf.at[core, rows, mine], True))
        for beside, part in others:
            out.append((at_side(gy=beside), block, buf.at[core, own, part], True))
            for side, source, rows in edges:
                target = buf.at[core, rows, part]
                out.append((at_side(gy=beside, gz=side), source, target, True))
        out.append(
            (at_side(gx=down), buf.at[2:4, own, mine], buf.at[2 + x : 4 + x, own, mine], False)
        )
        out.append((at_side(gx=up), buf.at[x : 2 + x, own, mine], buf.at[0:2, own, mine], False))
        return out

    def late(buf):
        low, high = slice(0, EDGE), slice(z + EDGE, full)
        from_low = (up, slice(x, 2 + x), slice(0, 2))
        from_high = (down, slice(2, 4), slice(2 + x, 4 + x))
        plan = []
        for _, part in others:
            plan.append((from_low, slice(0, full), part))
            plan += [(from_high, low, part), (from_high, high, part)]
        for side in (from_low, from_high):
            plan += [(side, low, mine), (side, high, mine)]
        return [
            (at_side(gx=side), buf.at[source, rows, part], buf.at[target, rows, part])
            for (side, source, target), rows, part in plan
        ]

    def forward(buf):
        planes = slice(2 + x, 4 + x)
        return [
            (at_side(gy=beside), buf.at[planes, own, mine], buf.at[planes, own, part])
            for beside, part in others
        ]

    others = [(up, slice(0, lanes))]
    if not wrap:
        others.append((down, slice(2 * lanes, 3 * lanes)))

    def remote(source, target, sems, number, device):
        return pltpu.make_async_remote_copy(
            src_ref=source,
            dst_ref=target,
            send_sem=sems[0].at[number],
            recv_sem=sems[1].at[number],
            device_id=device,
            device_id_type=MESH,
        )

    peers = []
    if inside:
        for dx in range(nx):
            for dy in range(ny):
                if dx or dy:
                    peers.append({"gx": lax.rem(ix + dx, nx), "gy": lax.rem(iy + dy, ny)})
    barrier = pltpu.get_barrier_semaphore()
    greeted = peers + [device for device, _, _, _ in early(eq)]
    for device in greeted:
        pl.semaphore_signal(barrier, inc=1, device_id=device, device_id_type=MESH)
    pl.semaphore_wait(barrier, len(greeted))

    if inside:
        copies = []
        for number, device in enumerate(peers):
            copy = remote(w_ref, wg.at[iy, ix], (wsend, wrecv), number, device)
            copy.start()
            copies.append(copy)
        wg[iy, ix] = w_ref[...]
        for copy in copies:
            copy.wait()
        ci = c // ny
        for which in range(2):
            for at in range(27):
                columns = []
                for j in range(ny):
                    pieces = [wg[j, i, which, :, at * ci : (at + 1) * ci] for i in range(nx)]
                    columns.append(jnp.concatenate(pieces, axis=0))
                wf[which, at // 3, at % 3] = jnp.concatenate(columns, axis=1)
        filters = wf
    else:
        filters = w_ref

    def exchange(buf, bank):
        sems = (send.at[bank], recv.at[bank])
        first, own_x = [], []
        number = 0
        for device, source, target, passed in early(buf):
            copy = remote(source, target, sems, number, device)
            number += 1
            copy.start()
            (first if passed else own_x).append(copy)
        for copy in first:
            copy.wait_recv()
        second = []
        for device, source, target in late(buf):
            copy = remote(source, target, sems, number, device)
            number += 1
            copy.start()
            second.append(copy)
        own_x[0].wait_recv()
        for device, source, target in forward(buf):
            copy = remote(source, target, sems, number, device)
            number += 1
            copy.start()
            second.append(copy)
        for copy in own_x[1:] + second:
            copy.wait_recv()
        for copy in first + own_x + second:
            copy.wait_send()

    def slot(at):
        return at % slots

    def unfold(tap, carry):
        blank = jnp.zeros((c, c), jnp.bfloat16)

        def rows(out, which, at, flip, cols, pick):
            line = [blank] * cols
            for col, b in pick:
                line[col] = filters[which, at, 2 - b if flip else b]
            return jnp.concatenate(line, axis=1)

        back = 8 - tap
        for yo in range(y + 2):
            a1[tap, yo * c : (yo + 1) * c, :] = rows(
                a1, 0, tap, False, slots, [(slot(yo + b), b) for b in range(3)]
            )
        for yo in range(y):
            a2[tap, yo * c : (yo + 1) * c, :] = rows(
                a2, 1, tap, False, y + 2, [(yo + b, b) for b in range(3)]
            )
        for s in range(slots):
            pick = [(yo, b) for yo in range(y + 2) for b in range(3) if slot(yo + b) == s]
            b2[tap, s * c : (s + 1) * c, :] = rows(b2, 1, back, True, y + 2, pick)
        for yi in range(y + 2):
            pick = [(yo, yi - yo) for yo in range(y) if 0 <= yi - yo <= 2]
            b1[tap, yi * c : (yi + 1) * c, :] = rows(b1, 0, back, True, y, pick)
        return carry

    lax.fori_loop(0, 9, unfold, 0)

    def load(ref2d, at):
        span = [ref2d[:, (at * y + j) * z : (at * y + j + 1) * z] for j in range(y)]
        return jnp.concatenate(span, axis=0).astype(jnp.float32).T

    for at in range(x):
        q_ref[at] = load(pos_ref, at)
        p_ref[at] = load(mom_ref, at)

    def conv(source, weights, out_x, transposed):
        width = source.shape[2]
        total = None
        for tz in range(3):
            part = None
            for tx in range(3):
                left = source[tx : tx + out_x].reshape(out_x * full, width)
                term = lax.dot_general(
                    left,
                    weights[tx * 3 + tz],
                    (((1,), (1 if transposed else 0,)), ((), ())),
                    preferred_element_type=jnp.float32,
                )
                part = term if part is None else part + term
            if tz != 1:
                part = pltpu.roll(part, 1 if tz == 0 else out_x * full - 1, 0)
            total = part if total is None else total + part
        return total.reshape(out_x, full, total.shape[-1])

    step = 0.25
    decay = jnp.exp(jnp.float32(-0.25))
    kick = jnp.sqrt(1.0 - decay * decay)

    def body(k, carry):
        eq[2 : 2 + x, own, mine] = q_ref[...].astype(jnp.bfloat16)
        exchange(eq, 0)
        t_ref[...] = jnp.tanh(conv(eq, a1, x + 2, True) + bias_ref[...][None])
        h2 = conv(t_ref[...].astype(jnp.bfloat16), a2, x, True)
        eh[2 : 2 + x, own, mine] = h2[:, own].astype(jnp.bfloat16)
        exchange(eh, 1)
        gu = conv(eh, b2, x + 2, False)
        t = t_ref[...]
        gh = (gu * (1.0 - t * t)).astype(jnp.bfloat16)
        force = conv(gh, b1, x, False)[:, own] + q_ref[...]
        half = 0.5 * step

        @pl.when(k > 0)
        def _():
            p_ref[...] = p_ref[...] - half * force

        @pl.when(k < steps)
        def _():
            p = p_ref[...] - half * force
            q = q_ref[...] + half * p
            now = noise_ref.at[k]
            drawn = jnp.stack([load(now, at) for at in range(x)])
            p = decay * p + kick * drawn
            q_ref[...] = q + half * p
            p_ref[...] = p

        return carry

    lax.fori_loop(0, steps + 1, body, 0)

    for ref, out in ((q_ref, q_out), (p_ref, p_out)):
        for at in range(x):
            flat = ref[at].T
            for j in range(y):
                out[:, (at * y + j) * z : (at * y + j + 1) * z] = flat[j * c : (j + 1) * c]


def on_device(sizes, position, momentum, noise, filter_in, filter_out, bias):
    nx, ny, nz = sizes
    c, x, y, z = position.shape
    steps = noise.shape[0]
    assert x >= 2 and y == 2 and z % EDGE == 0 and nx > 2 and ny > 1
    both = jnp.stack([filter_in, filter_out])
    co, ci = both.shape[1], both.shape[2]
    gather = []
    if co % EDGE == 0:
        both = both.transpose(0, 1, 3, 5, 4, 2).reshape(2, co, 27 * ci)
        gather = [
            pltpu.VMEM((ny, nx, 2, co, 27 * ci), jnp.bfloat16),
            pltpu.VMEM((2, 9, 3, c, c), jnp.bfloat16),
            pltpu.SemaphoreType.DMA((nx * ny - 1,)),
            pltpu.SemaphoreType.DMA((nx * ny - 1,)),
        ]
    else:
        both = both.reshape(2 * co, ci * 27)
        both = lax.all_gather(both, ("gx", "gy"), axis=0, tiled=True)
        both = both.reshape(nx, ny, 2, co, ci, 3, 3, 3)
        both = both.transpose(2, 5, 7, 6, 0, 3, 1, 4).reshape(2, 9, 3, c, c)
    lanes = y * c
    slots = 2 * y if ny == 2 else 3 * y
    full = z + 2 * EDGE
    wide = (y + 2) * c
    flat = jax.ShapeDtypeStruct((c, x * y * z), jnp.float32)
    copies = 15 if ny == 2 else 24
    vmem = pl.BlockSpec(memory_space=pltpu.VMEM)
    q, p = pl.pallas_call(
        functools.partial(kernel, steps, sizes),
        out_shape=(flat, flat),
        in_specs=[vmem] * 5,
        out_specs=(vmem, vmem),
        scratch_shapes=[
            pltpu.VMEM((9, wide, slots * c), jnp.bfloat16),
            pltpu.VMEM((9, lanes, wide), jnp.bfloat16),
            pltpu.VMEM((9, wide, lanes), jnp.bfloat16),
            pltpu.VMEM((9, slots * c, wide), jnp.bfloat16),
            pltpu.VMEM((x + 4, full, slots * c), jnp.bfloat16),
            pltpu.VMEM((x + 4, full, slots * c), jnp.bfloat16),
            pltpu.VMEM((x + 2, full, wide), jnp.float32),
            pltpu.VMEM((x, z, lanes), jnp.float32),
            pltpu.VMEM((x, z, lanes), jnp.float32),
            pltpu.SemaphoreType.DMA((2, copies)),
            pltpu.SemaphoreType.DMA((2, copies)),
            *gather,
        ],
        compiler_params=pltpu.CompilerParams(
            collective_id=0, has_side_effects=True, vmem_limit_bytes=56 * 2**20
        ),
    )(
        position.reshape(c, -1),
        momentum.reshape(c, -1),
        noise.reshape(steps, c, -1),
        both,
        jnp.tile(bias, y + 2)[None],
    )
    return q.reshape(position.shape), p.reshape(momentum.shape)


def solution(mesh):
    field = P(None, ("grp", "gx"), "gy", "gz")
    filters = P("gx", "gy", None, None, None)
    sizes = tuple(mesh.shape[name] for name in ("gx", "gy", "gz"))
    return jax.shard_map(
        functools.partial(on_device, sizes),
        mesh=mesh,
        in_specs=(field, field, P(None, None, ("grp", "gx"), "gy", "gz"), filters, filters, P()),
        out_specs=(field, field),
        check_vma=False,
    )
```

profile of v0, /device:TPU:0, one launch (start us, length us, event | category | flops | bytes accessed | tf_op | source)
XLA Modules:
  0.0 114.5 jit_solution(562578487603913163)
XLA Ops:
  0.6 1.0 maximum_bitcast_fusion
  1.6 0.1 copy.9
  1.8 0.0 copy-start
  1.8 0.8 reshape.26.w_ref
  2.6 0.1 copy-done
  2.7 0.0 copy-start.1
  2.7 0.7 reshape.25.noise_ref
  3.4 0.2 copy-done.1
  3.6 0.0 copy-start.2
  3.6 0.8 reshape.23.pos_ref
  4.4 0.1 copy-done.2
  4.5 0.0 copy-start.4
  4.5 0.8 reshape.24.mom_ref
  5.3 0.0 copy-done.4
  5.3 0.7 broadcast_in_dim_tile.3.bias_ref
  5.9 106.1 %shard_map.77 = (f32[64,512]{1,0:T(8,128)}, f32[64,512]{1,0:T(8,128)}) custom-call(f32[64,512]{1,0:T(8,128)} %reshape.23.pos_ref, f32[64,512]{1,0:T(8,128)} %reshape.24.mom_ref, bf16[3,64,512]{2,1,0:T(8,128)(2,1)} %reshape.25.noise_ref, bf16[2,16,864]{2,1,0:T(8,128)(2,1)} %reshape.26.w_ref, f32[1,256]{1,0:T(1,128)} %broadcast_in_dim_tile.3.bias_ref), custom_call_target="tpu_custom_call" | custom-call | tf_op jit(solution)/shard_map/pallas_call | solution.py:287
  112.1 0.0 copy-start.3
  112.1 1.7 %reshape.27 = f32[64,2,2,128]{3,2,1,0:T(2,128)} reshape(f32[64,512]{1,0:T(8,128)} %get-tuple-element.4) | data formatting | bytes 262144 | tf_op jit(solution)/shard_map/reshape | solution.py:316
  113.8 0.0 copy-done.3
  113.8 0.7 reshape.28
  (1 shorter events, 0.0 us)
Async XLA Ops:
  1.8 0.9 copy-start
  2.7 0.9 copy-start.1
  3.6 0.9 copy-start.2
  4.5 0.8 copy-start.4
  112.1 1.7 %copy-start.3 = (f32[64,512]{1,0:T(8,128)S(1)}, f32[64,512]{1,0:T(8,128)}, u32[]{:S(2)}) copy-start(f32[64,512]{1,0:T(8,128)} %get-tuple-element.5) | copy-start | bytes 393220
where the time goes:
time: 115 us; the launch traced here: 114 us
  Pallas kernels  106 us (92%)
  local copies, waits for them, and re-layouts  6.69 us (6%)
    pallas_call x1, Pallas kernels, on_device(): pl.pallas_call(functools.partial(kernel, steps, sizes), out_shape=(flat,...  106 us
    reshape x2, local copies, waits for them, and re-layouts, on_device(): return (q.reshape(position.shape), p.reshape(momentum.shape))  2.41 us

commit v1 on v0

--- a/solution.py
+++ b/solution.py
@@ -2,6 +2,7 @@
 
 import jax
 import jax.numpy as jnp
+import numpy as np
 from jax import lax
 from jax.experimental import pallas as pl
 from jax.experimental.pallas import tpu as pltpu
@@ -256,7 +257,419 @@
                 out[:, (at * y + j) * z : (at * y + j + 1) * z] = flat[j * c : (j + 1) * c]
 
 
+LANES = 128
+ROWS = 8
+
+
+def ring_place(r, nx):
+    row, step = r // nx, r % nx
+    return step + (row % 2) * (nx - 1 - 2 * step), row
+
+
+def ring_kernel(steps, sizes, pos_ref, mom_ref, noise_ref, fin_ref, fout_ref, bias_ref,
+                q_out, p_out, own_w, all_w, mats, turned, edges, msg0, got0, msgd, gotd,
+                stage, lhs, t_ref, base, extra, dq, dp, qb, halo, back_q, got_q, back_p, got_p,
+                send, recv):
+    nx, ny, nz = sizes
+    ring = nx * ny
+    x, zb = msg0.shape[1] - 1, msg0.shape[2]
+    lane = LANES
+    z = ring * zb
+    taps, co, ci = fin_ref.shape
+    c = ny * ci
+    y = lane // c
+    xx, yy = x * nx, y * ny
+    per = lane // ci
+    tiles = own_w.shape[0] // 2
+    wide = yy * c
+    reach = 4
+    rows = zb * xx
+
+    ix, iy, iz = lax.axis_index("gx"), lax.axis_index("gy"), lax.axis_index("gz")
+    me = iy * nx + ix + (iy % 2) * (nx - 1 - 2 * ix)
+
+    def device(r, core):
+        gx, gy = ring_place(r, nx)
+        return {"gx": gx, "gy": gy, "gz": core}
+
+    barrier = pltpu.get_barrier_semaphore()
+    everyone = 0
+    for dx in range(nx):
+        for dy in range(ny):
+            for dz in range(nz):
+                if dx or dy or dz:
+                    everyone += 1
+                    pl.semaphore_signal(
+                        barrier,
+                        inc=1,
+                        device_id={"gx": (ix + dx) % nx, "gy": (iy + dy) % ny, "gz": (iz + dz) % nz},
+                        device_id_type=MESH,
+                    )
+
+    def remote(source, target, number, where):
+        copy = pltpu.make_async_remote_copy(
+            src_ref=source,
+            dst_ref=target,
+            send_sem=send.at[number],
+            recv_sem=recv.at[number],
+            device_id=where,
+            device_id_type=MESH,
+        )
+        copy.start()
+        return copy
+
+    sent = []
+    used = [0]
+
+    def start(source, target, where):
+        copy = remote(source, target, used[0], where)
+        used[0] += 1
+        sent.append(copy)
+        return copy
+
+    def to_ring(source, target):
+        out = []
+        for j in range(1, ring):
+            r = (me + j) % ring
+            out.append(start(source(r), target, device(r, iz)))
+        return out
+
+    def arrive(copies):
+        for copy in copies:
+            copy.wait_recv()
+
+    for which, ref in enumerate((fin_ref, fout_ref)):
+        for tile in range(tiles):
+            parts = [ref[t].astype(jnp.float32) for t in range(tile * per, min(taps, (tile + 1) * per))]
+            parts += [jnp.zeros((co, ci), jnp.float32)] * (per - len(parts))
+            own_w[which * tiles + tile] = jnp.concatenate(parts, axis=1).astype(jnp.bfloat16)
+    first, second = (2 * tiles + 3) // 4, 0
+    second = tiles - first
+
+    def turn(ref, at):
+        parts = [ref[pl.ds(at * y + j, c, stride=x * y), :] for j in range(y)]
+        return jnp.concatenate(parts, axis=0).T
+
+    for at in range(x):
+        turned[at] = turn(pos_ref, at)
+
+    pl.semaphore_wait(barrier, everyone)
+
+    head = pl.ds(iz * first, first)
+    tail = pl.ds(2 * first + iz * second, second)
+    filters_a = to_ring(lambda r: own_w.at[head], all_w.at[me, head])
+    low = start(turned.at[:, z - ROWS : z], edges.at[0], {"gz": (iz + 1) % nz})
+    high = start(turned.at[:, 0:ROWS], edges.at[1], {"gz": (iz + nz - 1) % nz})
+    all_w[me, head] = own_w[head]
+    all_w[me, tail] = own_w[tail]
+
+    upper = lax.broadcasted_iota(jnp.int32, (ROWS, lane), 0) < reach
+    arrive([low, high])
+    for r in range(ring):
+        around = []
+        for at in range(x):
+            block = turned[at, r * zb : (r + 1) * zb]
+            msg0[r, at] = block.astype(jnp.bfloat16)
+            before = turned[at, r * zb - ROWS : r * zb] if r else edges[0, at]
+            after = turned[at, (r + 1) * zb : (r + 1) * zb + ROWS] if r < ring - 1 else edges[1, at]
+            around.append(jnp.where(upper, after, before))
+        msg0[r, x] = jnp.concatenate(around, axis=0).astype(jnp.bfloat16)
+    fields = to_ring(lambda r: msg0.at[r], got0.at[me])
+    got0[me] = msg0[me]
+    filters_b = to_ring(lambda r: own_w.at[tail], all_w.at[me, tail])
+
+    half = 0.125
+    decay = float(np.exp(np.float32(-0.25)))
+    kick = float(np.sqrt(np.float32(1.0) - np.exp(np.float32(-0.25)) ** 2))
+    push = half * (1.0 + decay)
+    q = pos_ref[...]
+    known = q.astype(jnp.bfloat16).astype(jnp.float32)
+    p = mom_ref[...] - half * q
+    total = x * y * c
+    drifts = []
+    for k in range(steps):
+        noise = noise_ref[k * total : (k + 1) * total].astype(jnp.float32)
+        q = q + push * p + (half * kick) * noise
+        drift = (q - known).astype(jnp.bfloat16).astype(jnp.float32)
+        known = known + drift
+        last = k == steps - 1
+        p = decay * p + kick * noise - (half if last else 2 * half) * q
+        q_out[...] = drift
+        for at in range(x):
+            flat = turn(q_out, at).astype(jnp.bfloat16)
+            for r in range(ring):
+                msgd[k, r, at] = flat[r * zb : (r + 1) * zb]
+        drifts.append(to_ring(lambda r: msgd.at[k, r], gotd.at[k, me]))
+        gotd[k, me] = msgd[k, me]
+    q_out[...] = q
+    p_out[...] = p
+
+    other = {"gz": (iz + 1) % nz}
+    arrive(filters_a)
+    swap_a = start(all_w.at[:, head], all_w.at[:, head], other)
+    at_lane = lax.broadcasted_iota(jnp.int32, (co, lane), 1)
+
+    def build(which):
+        def place(gx, carry):
+            row = pl.multiple_of(gx * co, co)
+            for a in range(3):
+                for cz in range(3):
+                    moved = {}
+                    for b in range(3):
+                        t = a * 9 + b * 3 + cz
+                        tile, spot = which * tiles + t // per, t % per
+                        for side in range(2):
+                            pieces = []
+                            for gy in range(ny):
+                                r = gy * nx + gx + (gy % 2) * (nx - 1 - 2 * gx)
+                                piece = all_w[r, tile].astype(jnp.float32)
+                                shift = (side * ny + gy - spot) % per
+                                pieces.append(pltpu.roll(piece, shift * ci, 1) if shift else piece)
+                            moved[b, side] = pieces
+                    pairs = []
+                    for b in range(yy):
+                        value = jnp.zeros((co, lane), jnp.float32)
+                        for side in range(y):
+                            near = (b + side) % yy
+                            if near > 2:
+                                continue
+                            for gy in range(ny):
+                                spot = (side * ny + gy) * ci
+                                inside = (at_lane >= spot) & (at_lane < spot + ci)
+                                value = jnp.where(inside, moved[near, side][gy], value)
+                        pairs.append(value.astype(jnp.bfloat16))
+                    for yo in range(yy):
+                        for h in range(yy // y):
+                            mats[which, a * 3 + cz, pl.ds(yo * c + row, co), h * lane : (h + 1) * lane] = (
+                                pairs[(h * y + 1 - yo) % yy]
+                            )
+            return carry
+
+        lax.fori_loop(0, nx, place, 0)
+
+    def scatter(target, zs, value, r, at):
+        gx, gy = ring_place(r, nx)
+        target[gy, pl.ds(zs * xx + gx * x + at, value.shape[0], stride=xx), :] = value
+
+    def whole(ref, rows_from, rows_to):
+        return jnp.concatenate([ref[gy, rows_from:rows_to] for gy in range(ny)], axis=1)
+
+    arrive(fields)
+    for r in range(ring):
+        around = got0[r, x].astype(jnp.float32)
+        for at in range(x):
+            scatter(stage, 0, got0[r, at].astype(jnp.float32), r, at)
+            scatter(stage, zb, around[at * ROWS : (at + 1) * ROWS], r, at)
+    base[...] = whole(stage, 0, rows)
+    arrive([swap_a])
+    build(0)
+    arrive(filters_b)
+    swap_b = start(all_w.at[:, tail], all_w.at[:, tail], other)
+
+    def spread(value):
+        n = value.shape[0]
+        cube = value.reshape(n // xx, xx, wide)
+        for a in range(3):
+            moved = cube if a == 1 else pltpu.roll(cube, (1 - a) % xx, 1)
+            moved = moved.reshape(n, wide)
+            lhs[a, 0, 0:n] = moved.astype(jnp.bfloat16)
+            lhs[a, 1, 0 : n - 2 * xx] = moved[xx : n - xx].astype(jnp.bfloat16)
+
+    def conv(which, n, adjoint):
+        out = None
+        for a in range(3):
+            for cz in range(3):
+                left = lhs[a, 1, 0:n] if cz == 1 else lhs[a, 0, cz * xx : cz * xx + n]
+                tap = a * 3 + cz
+                term = lax.dot_general(
+                    left,
+                    mats[which, 8 - tap if adjoint else tap],
+                    (((1,), (0 if adjoint else 1,)), ((), ())),
+                    preferred_element_type=jnp.float32,
+                )
+                out = term if out is None else out + term
+        return out
+
+    row = jnp.concatenate([bias_ref[...]] * yy, axis=1)
+
+    def gradient(between):
+        n = rows + 2 * (reach - 1) * xx
+        t = jnp.tanh(conv(0, n, False) + row)
+        t_ref[...] = t
+        spread(t)
+        between()
+        n -= 2 * xx
+        spread(conv(1, n, False))
+        n -= 2 * xx
+        gu = conv(1, n, True)
+        t = t_ref[2 * xx : 2 * xx + n]
+        spread(gu * (1.0 - t * t))
+        n -= 2 * xx
+        return conv(0, n, True)
+
+    def take_drift(k):
+        arrive(drifts[k])
+        for r in range(ring):
+            for at in range(x):
+                scatter(extra, 0, gotd[k, r, at].astype(jnp.float32), r, at)
+        base[...] = base[...] + whole(extra, 0, rows)
+
+    def second_filters():
+        arrive([swap_b])
+        build(1)
+
+    def collect(ref, r, at):
+        gx, gy = ring_place(r, nx)
+        return ref[gy, pl.ds(gx * x + at, zb, stride=xx), :]
+
+    def put(ref, value):
+        for gy in range(ny):
+            ref[gy] = value[:, gy * lane : (gy + 1) * lane]
+
+    turn_at = (zb + reach) * xx
+    field = [whole(stage, turn_at, turn_at + reach * xx), whole(stage, 0, turn_at)]
+    spread(jnp.concatenate(field, axis=0))
+    g = gradient(second_filters)
+    put(dp, -half * g)
+    put(dq, (-half * push) * g)
+    take_drift(0)
+
+    left_r, right_r = (me + ring - 1) % ring, (me + 1) % ring
+    left = device(left_r, (iz + nz - 1 + (me + ring - 1) // ring) % nz)
+    right = device(right_r, (iz + (me + 1) // ring) % nz)
+    edge = reach * xx
+    mine = pl.ds(pl.multiple_of(me * zb, zb), zb)
+    for k in range(1, steps + 1):
+        q = base[...] + whole(dq, 0, rows)
+        qb[k - 1] = q.astype(jnp.bfloat16)
+        below = start(qb.at[k - 1, rows - edge : rows], halo.at[k - 1, 0], right)
+        above = start(qb.at[k - 1, 0:edge], halo.at[k - 1, 1], left)
+        if k < steps:
+            take_drift(k)
+        else:
+            dp[...] = decay * dp[...] - half * dq[...]
+            for r in range(ring):
+                for at in range(x):
+                    back_q[r, at] = collect(dq, r, at)
+                    back_p[0, r, at] = collect(dp, r, at).astype(jnp.bfloat16)
+            sent_q = to_ring(lambda r: back_q.at[r], got_q.at[:, mine])
+            sent_p = to_ring(lambda r: back_p.at[0, r], got_p.at[0, :, mine])
+            got_q[:, mine] = back_q[me]
+            got_p[0, :, mine] = back_p[0, me]
+            dp[...] = dp[...] - dp[...].astype(jnp.bfloat16).astype(jnp.float32)
+        arrive([below, above])
+        spread(
+            jnp.concatenate(
+                [halo[k - 1, 0].astype(jnp.float32), q, halo[k - 1, 1].astype(jnp.float32)], axis=0
+            )
+        )
+        g = gradient(lambda: None)
+        if k < steps:
+            shift = whole(dq, 0, rows)
+            now = decay * whole(dp, 0, rows) - (2 * half) * (g + shift)
+            put(dp, now)
+            put(dq, shift + push * now)
+        else:
+            put(dp, whole(dp, 0, rows) - half * g)
+    for r in range(ring):
+        for at in range(x):
+            back_p[1, r, at] = collect(dp, r, at).astype(jnp.bfloat16)
+    last_p = to_ring(lambda r: back_p.at[1, r], got_p.at[1, :, mine])
+    got_p[1, :, mine] = back_p[1, me]
+
+    def untie(value, out, at):
+        flat = value.T
+        for j in range(y):
+            part = pl.ds(at * y + j, c, stride=x * y)
+            out[part, :] = out[part, :] + flat[j * c : (j + 1) * c]
+
+    arrive(sent_q)
+    for at in range(x):
+        untie(got_q[at], q_out, at)
+    arrive(sent_p)
+    arrive(last_p)
+    for at in range(x):
+        untie(got_p[0, at].astype(jnp.float32) + got_p[1, at].astype(jnp.float32), p_out, at)
+    for copy in sent:
+        copy.wait_send()
+
+
+def fits_ring(sizes, position, filter_in):
+    nx, ny, nz = sizes
+    c, x, y, z = position.shape
+    co, ci = filter_in.shape[:2]
+    ring = nx * ny
+    return (
+        nz == 2 and ny == 2 and nx > 1 and y * c == LANES and x * nx == ROWS and y * ny > 2
+        and z % (ring * EDGE) == 0 and z // ring == EDGE and co % EDGE == 0 and LANES % ci == 0
+        and y * ny * ci == LANES
+    )
+
+
+def on_ring(sizes, position, momentum, noise, filter_in, filter_out, bias):
+    nx, ny, nz = sizes
+    c, x, y, z = position.shape
+    steps = noise.shape[0]
+    co, ci = filter_in.shape[:2]
+    ring = nx * ny
+    zb = z // ring
+    xx, yy = x * nx, y * ny
+    wide = yy * c
+    rows = zb * xx
+    lane = LANES
+    tiles = -(-27 * ci // lane)
+    flat = jax.ShapeDtypeStruct((c * x * y, z), jnp.float32)
+    copies = (7 + steps) * (ring - 1) + 4 + 2 * steps
+    vmem = pl.BlockSpec(memory_space=pltpu.VMEM)
+    bf16, f32 = jnp.bfloat16, jnp.float32
+    q, p = pl.pallas_call(
+        functools.partial(ring_kernel, steps, sizes),
+        out_shape=(flat, flat),
+        in_specs=[vmem] * 6,
+        out_specs=(vmem, vmem),
+        scratch_shapes=[
+            pltpu.VMEM((2 * tiles, co, lane), bf16),
+            pltpu.VMEM((ring, 2 * tiles, co, lane), bf16),
+            pltpu.VMEM((2, 9, wide, wide), bf16),
+            pltpu.VMEM((x, z, lane), f32),
+            pltpu.VMEM((2, x, ROWS, lane), f32),
+            pltpu.VMEM((ring, x + 1, zb, lane), bf16),
+            pltpu.VMEM((ring, x + 1, zb, lane), bf16),
+            pltpu.VMEM((steps, ring, x, zb, lane), bf16),
+            pltpu.VMEM((steps, ring, x, zb, lane), bf16),
+            pltpu.VMEM((ny, rows + ROWS * xx, lane), f32),
+            pltpu.VMEM((3, 2, rows + ROWS * xx, wide), bf16),
+            pltpu.VMEM((rows + 6 * xx, wide), f32),
+            pltpu.VMEM((rows, wide), f32),
+            pltpu.VMEM((ny, rows, lane), f32),
+            pltpu.VMEM((ny, rows, lane), f32),
+            pltpu.VMEM((ny, rows, lane), f32),
+            pltpu.VMEM((steps, rows, wide), bf16),
+            pltpu.VMEM((steps, 2, 4 * xx, wide), bf16),
+            pltpu.VMEM((ring, x, zb, lane), f32),
+            pltpu.VMEM((x, z, lane), f32),
+            pltpu.VMEM((2, ring, x, zb, lane), bf16),
+            pltpu.VMEM((2, x, z, lane), bf16),
+            pltpu.SemaphoreType.DMA((copies,)),
+            pltpu.SemaphoreType.DMA((copies,)),
+        ],
+        compiler_params=pltpu.CompilerParams(
+            collective_id=0, has_side_effects=True, vmem_limit_bytes=56 * 2**20
+        ),
+    )(
+        position.reshape(-1, z),
+        momentum.reshape(-1, z),
+        noise.reshape(-1, z),
+        filter_in.transpose(2, 3, 4, 0, 1).reshape(27, co, ci),
+        filter_out.transpose(2, 3, 4, 0, 1).reshape(27, co, ci),
+        bias[None],
+    )
+    return q.reshape(position.shape), p.reshape(momentum.shape)
+
+
 def on_device(sizes, position, momentum, noise, filter_in, filter_out, bias):
+    if fits_ring(sizes, position, filter_in):
+        return on_ring(sizes, position, momentum, noise, filter_in, filter_out, bias)
     nx, ny, nz = sizes
     c, x, y, z = position.shape
     steps = noise.shape[0]

time: 115 us -> 46.6 us (0.41)
  Pallas kernels: 106 us -> 43.5 us
  local copies, waits for them, and re-layouts: 6.69 us -> 2.26 us
    pallas_call x1, Pallas kernels: 106 us -> 43.5 us  [on_ring(): pl.pallas_call(functools.partial(ring_kernel, steps, sizes), out_shape=(f...]
    reshape x6 -> x0, local copies, waits for them, and re-layouts: 5.49 us -> none  [the longest x2 2.41 us: on_device(): return (q.reshape(position.shape), p.reshape(momentum.shape))]
    unnamed x10 -> x4, local copies, waits for them, and re-layouts: 0.41 us -> 2.26 us
where the time goes in v1:
time: 46.6 us; the launch traced here: 46.5 us
  Pallas kernels  43.5 us (93%)
  local copies, waits for them, and re-layouts  2.26 us (5%)
  between operations  0.65 us (1%)
    pallas_call x1, Pallas kernels, on_ring(): pl.pallas_call(functools.partial(ring_kernel, steps, sizes), out_shape=(f...  43.5 us
    unnamed x4, local copies, waits for them, and re-layouts  2.26 us

profile of v1, /device:TPU:0, one launch (start us, length us, event | category | flops | bytes accessed | tf_op | source)
XLA Modules:
  0.0 46.5 jit_solution(16623169140719105970)
XLA Ops:
  0.6 43.5 %shard_map.77 = (f32[256,128]{1,0:T(8,128)}, f32[256,128]{1,0:T(8,128)}) custom-call(f32[256,128]{1,0:T(8,128)} %bitcast.15, f32[256,128]{1,0:T(8,128)} %bitcast.16, bf16[768,128]{1,0:T(8,128)(2,1)} %bitcast.12, bf16[27,16,32]{2,1,0:T(8,128)(2,1)} %bitcast.17, bf16[27,16,32]{2,1,0:T(8,128)(2,1)} %bitcast.18, f32[1,64]{1,0:T(1,128)} %bitcast.19), custom_call_target="tpu_custom_call" | custom-call | tf_op jit(solution)/shard_map/pallas_call | solution.py:625
  44.2 0.0 copy-start
  44.2 1.6 %copy.10 = f32[64,2,2,128]{3,2,1,0:T(2,128)} copy(f32[64,2,2,128]{3,2,1,0:T(2,128)} %bitcast.14) | data formatting | bytes 262144
  45.8 0.0 copy-done
  45.8 0.7 %copy.11 = f32[64,2,2,128]{3,2,1,0:T(2,128)} copy(f32[64,2,2,128]{3,2,1,0:T(2,128)S(1)} %bitcast.13) | data formatting | bytes 262144
Async XLA Ops:
  44.2 1.6 %copy-start = (f32[256,128]{1,0:T(8,128)S(1)}, f32[256,128]{1,0:T(8,128)}, u32[]{:S(2)}) copy-start(f32[256,128]{1,0:T(8,128)} %get-tuple-element.5) | copy-start | bytes 393220

commit v2 on v1

--- a/solution.py
+++ b/solution.py
@@ -266,11 +266,27 @@
     return step + (row % 2) * (nx - 1 - 2 * step), row
 
 
-def ring_kernel(steps, sizes, pos_ref, mom_ref, noise_ref, fin_ref, fout_ref, bias_ref,
-                q_out, p_out, own_w, all_w, mats, turned, edges, msg0, got0, msgd, gotd,
-                stage, lhs, t_ref, base, extra, dq, dp, qb, halo, back_q, got_q, back_p, got_p,
-                send, recv):
+def ring_kernel(steps, sizes, heights, *refs):
+    accs = []
+    for unit in range(2):
+        for height in heights:
+            low = -(-height // (2 * EDGE)) * EDGE
+            for part in (low, height - low):
+                accs.append(pltpu.ACC(unit)((part, 2 * LANES), jnp.float32))
+    pl.run_scoped(functools.partial(ring_body, steps, sizes, refs), *accs)
+
+
+def ring_body(steps, sizes, refs, *sums):
     nx, ny, nz = sizes
+    count = len(sums) // 2
+    accs = [
+        [[sums[unit * count + 2 * place + part] for part in range(2)] for unit in range(2)]
+        for place in range(count // 2)
+    ]
+    inputs, refs = refs[:6], refs[6:]
+    (q_out, p_out, pos_ref, mom_ref, noise_ref, fin_ref, fout_ref, bias_ref, own_w, all_w, mats,
+     flipped, turned, edges, msg0, got0, msgd, gotd, stage, lhs, t_ref, base, extra, dq, dp, qb,
+     halo, back_q, got_q, back_p, got_p, fixed, loose, send, recv, load) = refs
     ring = nx * ny
     x, zb = msg0.shape[1] - 1, msg0.shape[2]
     lane = LANES
@@ -306,6 +322,13 @@
                         device_id_type=MESH,
                     )
 
+    loads = []
+    held = (pos_ref, mom_ref, noise_ref, fin_ref, fout_ref, bias_ref)
+    for number in (3, 4, 0, 1, 2, 5):
+        copy = pltpu.make_async_copy(inputs[number], held[number], load.at[number])
+        copy.start()
+        loads.append(copy)
+
     def remote(source, target, number, where):
         copy = pltpu.make_async_remote_copy(
             src_ref=source,
@@ -338,6 +361,8 @@
         for copy in copies:
             copy.wait_recv()
 
+    loads[0].wait()
+    loads[1].wait()
     for which, ref in enumerate((fin_ref, fout_ref)):
         for tile in range(tiles):
             parts = [ref[t].astype(jnp.float32) for t in range(tile * per, min(taps, (tile + 1) * per))]
@@ -350,16 +375,36 @@
         parts = [ref[pl.ds(at * y + j, c, stride=x * y), :] for j in range(y)]
         return jnp.concatenate(parts, axis=0).T
 
+    loads[2].wait()
     for at in range(x):
         turned[at] = turn(pos_ref, at)
 
+    for each in sums:
+        pltpu.matmul_pop(each)
+
     pl.semaphore_wait(barrier, everyone)
 
     head = pl.ds(iz * first, first)
     tail = pl.ds(2 * first + iz * second, second)
-    filters_a = to_ring(lambda r: own_w.at[head], all_w.at[me, head])
+    beside = {"gy": (iy + 1) % ny}
+
+    def to_column(part):
+        out = []
+        for dx in range(1, nx):
+            out.append(start(own_w.at[part], all_w.at[me, part], {"gx": (ix + dx) % nx}))
+        return out, [start(own_w.at[part], all_w.at[me, part], beside)]
+
+    def pass_on(part, column, across):
+        for dx in range(1, nx):
+            arrive([column[dx - 1]])
+            gx = (ix + nx - dx) % nx
+            r = iy * nx + gx + (iy % 2) * (nx - 1 - 2 * gx)
+            across.append(start(all_w.at[r, part], all_w.at[r, part], beside))
+
+    column_a, across_a = to_column(head)
     low = start(turned.at[:, z - ROWS : z], edges.at[0], {"gz": (iz + 1) % nz})
     high = start(turned.at[:, 0:ROWS], edges.at[1], {"gz": (iz + nz - 1) % nz})
+    column_b, across_b = to_column(tail)
     all_w[me, head] = own_w[head]
     all_w[me, tail] = own_w[tail]
 
@@ -376,12 +421,14 @@
         msg0[r, x] = jnp.concatenate(around, axis=0).astype(jnp.bfloat16)
     fields = to_ring(lambda r: msg0.at[r], got0.at[me])
     got0[me] = msg0[me]
-    filters_b = to_ring(lambda r: own_w.at[tail], all_w.at[me, tail])
 
     half = 0.125
     decay = float(np.exp(np.float32(-0.25)))
     kick = float(np.sqrt(np.float32(1.0) - np.exp(np.float32(-0.25)) ** 2))
     push = half * (1.0 + decay)
+    loads[3].wait()
+    loads[4].wait()
+    loads[5].wait()
     q = pos_ref[...]
     known = q.astype(jnp.bfloat16).astype(jnp.float32)
     p = mom_ref[...] - half * q
@@ -394,18 +441,22 @@
         known = known + drift
         last = k == steps - 1
         p = decay * p + kick * noise - (half if last else 2 * half) * q
-        q_out[...] = drift
+        loose[k] = drift
         for at in range(x):
-            flat = turn(q_out, at).astype(jnp.bfloat16)
+            flat = turn(loose.at[k], at).astype(jnp.bfloat16)
             for r in range(ring):
                 msgd[k, r, at] = flat[r * zb : (r + 1) * zb]
+        gotd[k, me] = msgd[k, me]
+    fixed[0] = q
+    fixed[1] = p
+
+    def send_drift(k):
         drifts.append(to_ring(lambda r: msgd.at[k, r], gotd.at[k, me]))
-        gotd[k, me] = msgd[k, me]
-    q_out[...] = q
-    p_out[...] = p
 
     other = {"gz": (iz + 1) % nz}
-    arrive(filters_a)
+    pass_on(head, column_a, across_a)
+    pass_on(tail, column_b, across_b)
+    arrive(across_a)
     swap_a = start(all_w.at[:, head], all_w.at[:, head], other)
     at_lane = lax.broadcasted_iota(jnp.int32, (co, lane), 1)
 
@@ -447,6 +498,10 @@
 
         lax.fori_loop(0, nx, place, 0)
 
+    def turn_over(which):
+        for tap in range(9):
+            flipped[which, tap] = mats[which, tap].T
+
     def scatter(target, zs, value, r, at):
         gx, gy = ring_place(r, nx)
         target[gy, pl.ds(zs * xx + gx * x + at, value.shape[0], stride=xx), :] = value
@@ -454,17 +509,19 @@
     def whole(ref, rows_from, rows_to):
         return jnp.concatenate([ref[gy, rows_from:rows_to] for gy in range(ny)], axis=1)
 
+    arrive([swap_a])
+    build(0)
+    arrive(across_b)
+    swap_b = start(all_w.at[:, tail], all_w.at[:, tail], other)
+    turn_over(0)
     arrive(fields)
+    send_drift(0)
     for r in range(ring):
         around = got0[r, x].astype(jnp.float32)
         for at in range(x):
             scatter(stage, 0, got0[r, at].astype(jnp.float32), r, at)
             scatter(stage, zb, around[at * ROWS : (at + 1) * ROWS], r, at)
     base[...] = whole(stage, 0, rows)
-    arrive([swap_a])
-    build(0)
-    arrive(filters_b)
-    swap_b = start(all_w.at[:, tail], all_w.at[:, tail], other)
 
     def spread(value):
         n = value.shape[0]
@@ -475,37 +532,48 @@
             lhs[a, 0, 0:n] = moved.astype(jnp.bfloat16)
             lhs[a, 1, 0 : n - 2 * xx] = moved[xx : n - xx].astype(jnp.bfloat16)
 
-    def conv(which, n, adjoint):
-        out = None
-        for a in range(3):
-            for cz in range(3):
-                left = lhs[a, 1, 0:n] if cz == 1 else lhs[a, 0, cz * xx : cz * xx + n]
-                tap = a * 3 + cz
-                term = lax.dot_general(
-                    left,
-                    mats[which, 8 - tap if adjoint else tap],
-                    (((1,), (0 if adjoint else 1,)), ((), ())),
-                    preferred_element_type=jnp.float32,
+    def conv(place, which, adjoint, flip=False):
+        source = mats if adjoint or flip else flipped
+        sums = accs[place]
+        low, high = sums[0][0].shape[0], sums[0][1].shape[0]
+        plans = (
+            [(0, True, True), (1, True, True), (2, True, True), (3, True, True), (4, True, False)],
+            [(8, True, True), (7, True, True), (6, True, True), (5, True, True), (4, False, True)],
+        )
+        for at in range(5):
+            for unit in range(2):
+                tap, use_low, use_high = plans[unit][at]
+                a, cz = tap // 3, tap % 3
+                pltpu.matmul_push_rhs(
+                    source[which, 8 - tap if adjoint else tap],
+                    staging_register=at % 2,
+                    mxu_index=unit,
+                    transpose=flip,
                 )
-                out = term if out is None else out + term
-        return out
+                copy, first_row = (1, 0) if cz == 1 else (0, cz * xx)
+                fresh = at % 2
+                if use_low:
+                    left = lhs[a, copy, first_row : first_row + low]
+                    pltpu.matmul_acc_lhs(sums[unit][0], left, load_staged_rhs=fresh)
+                    fresh = None
+                if use_high:
+                    left = lhs[a, copy, first_row + low : first_row + low + high]
+                    pltpu.matmul_acc_lhs(sums[unit][1], left, load_staged_rhs=fresh)
+        halves = [pltpu.matmul_pop(sums[0][part]) + pltpu.matmul_pop(sums[1][part]) for part in range(2)]
+        return jnp.concatenate(halves, axis=0)
 
     row = jnp.concatenate([bias_ref[...]] * yy, axis=1)
 
-    def gradient(between):
-        n = rows + 2 * (reach - 1) * xx
-        t = jnp.tanh(conv(0, n, False) + row)
+    def gradient(between, flip=False):
+        t = jnp.tanh(conv(0, 0, False) + row)
         t_ref[...] = t
         spread(t)
         between()
-        n -= 2 * xx
-        spread(conv(1, n, False))
-        n -= 2 * xx
-        gu = conv(1, n, True)
-        t = t_ref[2 * xx : 2 * xx + n]
+        spread(conv(1, 1, False, flip))
+        gu = conv(2, 1, True)
+        t = t_ref[2 * xx : 2 * xx + gu.shape[0]]
         spread(gu * (1.0 - t * t))
-        n -= 2 * xx
-        return conv(0, n, True)
+        return conv(3, 0, True)
 
     def take_drift(k):
         arrive(drifts[k])
@@ -516,6 +584,7 @@
 
     def second_filters():
         arrive([swap_b])
+        send_drift(1)
         build(1)
 
     def collect(ref, r, at):
@@ -529,7 +598,7 @@
     turn_at = (zb + reach) * xx
     field = [whole(stage, turn_at, turn_at + reach * xx), whole(stage, 0, turn_at)]
     spread(jnp.concatenate(field, axis=0))
-    g = gradient(second_filters)
+    g = gradient(second_filters, True)
     put(dp, -half * g)
     put(dq, (-half * push) * g)
     take_drift(0)
@@ -544,6 +613,10 @@
         qb[k - 1] = q.astype(jnp.bfloat16)
         below = start(qb.at[k - 1, rows - edge : rows], halo.at[k - 1, 0], right)
         above = start(qb.at[k - 1, 0:edge], halo.at[k - 1, 1], left)
+        if k == 1:
+            for later in range(2, steps):
+                send_drift(later)
+            turn_over(1)
         if k < steps:
             take_drift(k)
         else:
@@ -577,19 +650,19 @@
     last_p = to_ring(lambda r: back_p.at[1, r], got_p.at[1, :, mine])
     got_p[1, :, mine] = back_p[1, me]
 
-    def untie(value, out, at):
+    def untie(value, which, out, at):
         flat = value.T
         for j in range(y):
             part = pl.ds(at * y + j, c, stride=x * y)
-            out[part, :] = out[part, :] + flat[j * c : (j + 1) * c]
+            out[part, :] = fixed[which, part, :] + flat[j * c : (j + 1) * c]
 
     arrive(sent_q)
     for at in range(x):
-        untie(got_q[at], q_out, at)
+        untie(got_q[at], 0, q_out, at)
     arrive(sent_p)
     arrive(last_p)
     for at in range(x):
-        untie(got_p[0, at].astype(jnp.float32) + got_p[1, at].astype(jnp.float32), p_out, at)
+        untie(got_p[0, at].astype(jnp.float32) + got_p[1, at].astype(jnp.float32), 1, p_out, at)
     for copy in sent:
         copy.wait_send()
 
@@ -619,17 +692,25 @@
     lane = LANES
     tiles = -(-27 * ci // lane)
     flat = jax.ShapeDtypeStruct((c * x * y, z), jnp.float32)
-    copies = (7 + steps) * (ring - 1) + 4 + 2 * steps
+    copies = (4 + steps) * (ring - 1) + 4 * nx + 4 + 2 * steps
+    heights = [(zb + 2 * reach) * xx for reach in (3, 2, 1, 0)]
     vmem = pl.BlockSpec(memory_space=pltpu.VMEM)
     bf16, f32 = jnp.bfloat16, jnp.float32
     q, p = pl.pallas_call(
-        functools.partial(ring_kernel, steps, sizes),
+        functools.partial(ring_kernel, steps, sizes, heights),
         out_shape=(flat, flat),
-        in_specs=[vmem] * 6,
+        in_specs=[pl.BlockSpec(memory_space=pl.ANY)] * 6,
         out_specs=(vmem, vmem),
         scratch_shapes=[
+            pltpu.VMEM((c * x * y, z), f32),
+            pltpu.VMEM((c * x * y, z), f32),
+            pltpu.VMEM((steps * c * x * y, z), bf16),
+            pltpu.VMEM((27, co, ci), bf16),
+            pltpu.VMEM((27, co, ci), bf16),
+            pltpu.VMEM((1, c), f32),
             pltpu.VMEM((2 * tiles, co, lane), bf16),
             pltpu.VMEM((ring, 2 * tiles, co, lane), bf16),
+            pltpu.VMEM((2, 9, wide, wide), bf16),
             pltpu.VMEM((2, 9, wide, wide), bf16),
             pltpu.VMEM((x, z, lane), f32),
             pltpu.VMEM((2, x, ROWS, lane), f32),
@@ -650,19 +731,27 @@
             pltpu.VMEM((x, z, lane), f32),
             pltpu.VMEM((2, ring, x, zb, lane), bf16),
             pltpu.VMEM((2, x, z, lane), bf16),
+            pltpu.VMEM((2, c * x * y, z), f32),
+            pltpu.VMEM((steps, c * x * y, z), f32),
             pltpu.SemaphoreType.DMA((copies,)),
             pltpu.SemaphoreType.DMA((copies,)),
+            pltpu.SemaphoreType.DMA((6,)),
         ],
         compiler_params=pltpu.CompilerParams(
-            collective_id=0, has_side_effects=True, vmem_limit_bytes=56 * 2**20
+            collective_id=0, has_side_effects=True, vmem_limit_bytes=24 * 2**20
         ),
     )(
-        position.reshape(-1, z),
-        momentum.reshape(-1, z),
-        noise.reshape(-1, z),
-        filter_in.transpose(2, 3, 4, 0, 1).reshape(27, co, ci),
-        filter_out.transpose(2, 3, 4, 0, 1).reshape(27, co, ci),
-        bias[None],
+        *(
+            pltpu.with_memory_space_constraint(each, pltpu.HBM)
+            for each in (
+                position.reshape(-1, z),
+                momentum.reshape(-1, z),
+                noise.reshape(-1, z),
+                filter_in.transpose(2, 3, 4, 0, 1).reshape(27, co, ci),
+                filter_out.transpose(2, 3, 4, 0, 1).reshape(27, co, ci),
+                bias[None],
+            )
+        )
     )
     return q.reshape(position.shape), p.reshape(momentum.shape)
 

time: 46.6 us -> 39.4 us (0.85)
  Pallas kernels: 43.5 us -> 37.3 us
  local copies, waits for them, and re-layouts: 2.26 us -> 1.31 us
    pallas_call x1, Pallas kernels: 43.5 us -> 37.3 us  [on_ring(): pl.pallas_call(functools.partial(ring_kernel, steps, sizes, heights), out...]
    unnamed x4 -> x2, local copies, waits for them, and re-layouts: 2.26 us -> 1.31 us
where the time goes in v2:
time: 39.4 us; the launch traced here: 39.2 us
  Pallas kernels  37.3 us (95%)
  local copies, waits for them, and re-layouts  1.31 us (3%)
  between operations  0.64 us (2%)
    pallas_call x1, Pallas kernels, on_ring(): pl.pallas_call(functools.partial(ring_kernel, steps, sizes, heights), out...  37.3 us
    unnamed x2, local copies, waits for them, and re-layouts  1.31 us

profile of v2, /device:TPU:0, one launch (start us, length us, event | category | flops | bytes accessed | tf_op | source)
XLA Modules:
  0.0 39.2 jit_solution(11084310310025670394)
XLA Ops:
  0.6 37.3 %shard_map.77 = (f32[256,128]{1,0:T(8,128)S(1)}, f32[256,128]{1,0:T(8,128)S(1)}) custom-call(f32[256,128]{1,0:T(8,128)} %bitcast.15, f32[256,128]{1,0:T(8,128)} %bitcast.16, bf16[768,128]{1,0:T(8,128)(2,1)} %bitcast.14, bf16[27,16,32]{2,1,0:T(8,128)(2,1)} %bitcast.17, bf16[27,16,32]{2,1,0:T(8,128)(2,1)} %bitcast.18, f32[1,64]{1,0:T(1,128)} %bitcast.19), custom_call_target="tpu_custom_call" | custom-call | tf_op jit(solution)/shard_map/pallas_call | solution.py:699
  37.9 0.7 %copy.10 = f32[64,2,2,128]{3,2,1,0:T(2,128)} copy(f32[64,2,2,128]{3,2,1,0:T(2,128)S(1)} %bitcast.13) | data formatting | bytes 262144
  38.6 0.7 %copy.11 = f32[64,2,2,128]{3,2,1,0:T(2,128)} copy(f32[64,2,2,128]{3,2,1,0:T(2,128)S(1)} %bitcast.12) | data formatting | bytes 262144

commit v3 on v2

--- a/solution.py
+++ b/solution.py
@@ -296,13 +296,16 @@
     y = lane // c
     xx, yy = x * nx, y * ny
     per = lane // ci
-    tiles = own_w.shape[0] // 2
+    tiles = own_w.shape[1]
     wide = yy * c
     reach = 4
     rows = zb * xx
 
     ix, iy, iz = lax.axis_index("gx"), lax.axis_index("gy"), lax.axis_index("gz")
     me = iy * nx + ix + (iy % 2) * (nx - 1 - 2 * ix)
+    block = nz * me + iz
+    home = block // ring == iz
+    filed = block % ring
 
     def device(r, core):
         gx, gy = ring_place(r, nx)
@@ -329,8 +332,8 @@
         copy.start()
         loads.append(copy)
 
-    def remote(source, target, number, where):
-        copy = pltpu.make_async_remote_copy(
+    def copy_of(source, target, number, where):
+        return pltpu.make_async_remote_copy(
             src_ref=source,
             dst_ref=target,
             send_sem=send.at[number],
@@ -338,38 +341,70 @@
             device_id=where,
             device_id_type=MESH,
         )
-        copy.start()
-        return copy
-
-    sent = []
-    used = [0]
-
-    def start(source, target, where):
-        copy = remote(source, target, used[0], where)
-        used[0] += 1
-        sent.append(copy)
-        return copy
-
-    def to_ring(source, target):
-        out = []
-        for j in range(1, ring):
+
+    across = {"gy": (iy + 1) % ny}
+    other = {"gz": (iz + 1) % nz}
+
+    def start(source, target, number, where):
+        copy_of(source, target, number, where).start()
+
+    def arrive(number, like):
+        copy_of(like, like, number, other).wait_recv()
+
+    def leave(number, like):
+        copy_of(like, like, number, other).wait_send()
+
+    def start_or_keep(source, target, number, where):
+        @pl.when(home)
+        def _():
+            pltpu.make_async_copy(source, target, recv.at[number]).start()
+
+        @pl.when(jnp.logical_not(home))
+        def _():
+            start(source, target, number, where)
+
+    def to_owners(buf, target, number):
+        for j in range(1, ring + 1):
+            at = (filed + j) % ring
+            owner = iz * ring + at
+            go = start if j < ring else start_or_keep
+            go(buf.at[at], target, number, device(owner // nz, owner % nz))
+
+    def to_sources(buf, target, number):
+        for j in range(1, ring + 1):
             r = (me + j) % ring
-            out.append(start(source(r), target, device(r, iz)))
-        return out
-
-    def arrive(copies):
-        for copy in copies:
-            copy.wait_recv()
-
+            go = start if j < ring else start_or_keep
+            go(buf.at[r], target, number, device(r, block // ring))
+
+    def left_ring(number, buf):
+        @pl.when(home)
+        def _():
+            leave(number, buf.at[0 : ring - 1])
+
+        @pl.when(jnp.logical_not(home))
+        def _():
+            leave(number, buf)
+
+    column_sems = [[which * (nx - 1) + dx for dx in range(nx - 1)] for which in range(2)]
+    across_sem = [2 * (nx - 1), 2 * (nx - 1) + 1]
+    swap_sem = [2 * nx, 2 * nx + 1]
+    edge_sem, field_sem = 2 * nx + 2, 2 * nx + 3
+    drift_sem = [2 * nx + 4 + k for k in range(steps)]
+    halo_sem = [2 * nx + 4 + steps + k for k in range(steps)]
+    q_sem, p_sem = 2 * nx + 4 + 2 * steps, [2 * nx + 5 + 2 * steps, 2 * nx + 6 + 2 * steps]
+
+    outer = iz == nz - 1
     loads[0].wait()
     loads[1].wait()
-    for which, ref in enumerate((fin_ref, fout_ref)):
-        for tile in range(tiles):
-            parts = [ref[t].astype(jnp.float32) for t in range(tile * per, min(taps, (tile + 1) * per))]
-            parts += [jnp.zeros((co, ci), jnp.float32)] * (per - len(parts))
-            own_w[which * tiles + tile] = jnp.concatenate(parts, axis=1).astype(jnp.bfloat16)
-    first, second = (2 * tiles + 3) // 4, 0
-    second = tiles - first
+
+    @pl.when(outer)
+    def _():
+        for which, ref in enumerate((fin_ref, fout_ref)):
+            for tile in range(tiles):
+                span = range(tile * per, min(taps, (tile + 1) * per))
+                parts = [ref[t].astype(jnp.float32) for t in span]
+                parts += [jnp.zeros((co, ci), jnp.float32)] * (per - len(parts))
+                own_w[which, tile] = jnp.concatenate(parts, axis=1).astype(jnp.bfloat16)
 
     def turn(ref, at):
         parts = [ref[pl.ds(at * y + j, c, stride=x * y), :] for j in range(y)]
@@ -384,43 +419,42 @@
 
     pl.semaphore_wait(barrier, everyone)
 
-    head = pl.ds(iz * first, first)
-    tail = pl.ds(2 * first + iz * second, second)
-    beside = {"gy": (iy + 1) % ny}
-
-    def to_column(part):
-        out = []
+    def to_column(which):
         for dx in range(1, nx):
-            out.append(start(own_w.at[part], all_w.at[me, part], {"gx": (ix + dx) % nx}))
-        return out, [start(own_w.at[part], all_w.at[me, part], beside)]
-
-    def pass_on(part, column, across):
+            there = {"gx": (ix + dx) % nx}
+            start(own_w.at[which], all_w.at[which, me], column_sems[which][dx - 1], there)
+        start(own_w.at[which], all_w.at[which, me], across_sem[which], across)
+
+    def pass_on(which):
         for dx in range(1, nx):
-            arrive([column[dx - 1]])
+            arrive(column_sems[which][dx - 1], own_w.at[which])
             gx = (ix + nx - dx) % nx
             r = iy * nx + gx + (iy % 2) * (nx - 1 - 2 * gx)
-            across.append(start(all_w.at[r, part], all_w.at[r, part], beside))
-
-    column_a, across_a = to_column(head)
-    low = start(turned.at[:, z - ROWS : z], edges.at[0], {"gz": (iz + 1) % nz})
-    high = start(turned.at[:, 0:ROWS], edges.at[1], {"gz": (iz + nz - 1) % nz})
-    column_b, across_b = to_column(tail)
-    all_w[me, head] = own_w[head]
-    all_w[me, tail] = own_w[tail]
+            start(all_w.at[which, r], all_w.at[which, r], across_sem[which], across)
+
+    @pl.when(outer)
+    def _():
+        to_column(0)
+
+    start(turned.at[:, z - ROWS : z], edges.at[0], edge_sem, {"gz": (iz + 1) % nz})
+    start(turned.at[:, 0:ROWS], edges.at[1], edge_sem, {"gz": (iz + nz - 1) % nz})
+
+    @pl.when(outer)
+    def _():
+        to_column(1)
+        all_w[:, me] = own_w[...]
 
     upper = lax.broadcasted_iota(jnp.int32, (ROWS, lane), 0) < reach
-    arrive([low, high])
+    arrive(edge_sem, edges)
     for r in range(ring):
         around = []
         for at in range(x):
-            block = turned[at, r * zb : (r + 1) * zb]
-            msg0[r, at] = block.astype(jnp.bfloat16)
+            msg0[r, at] = turned[at, r * zb : (r + 1) * zb].astype(jnp.bfloat16)
             before = turned[at, r * zb - ROWS : r * zb] if r else edges[0, at]
             after = turned[at, (r + 1) * zb : (r + 1) * zb + ROWS] if r < ring - 1 else edges[1, at]
             around.append(jnp.where(upper, after, before))
         msg0[r, x] = jnp.concatenate(around, axis=0).astype(jnp.bfloat16)
-    fields = to_ring(lambda r: msg0.at[r], got0.at[me])
-    got0[me] = msg0[me]
+    to_owners(msg0, got0.at[me], field_sem)
 
     half = 0.125
     decay = float(np.exp(np.float32(-0.25)))
@@ -433,7 +467,6 @@
     known = q.astype(jnp.bfloat16).astype(jnp.float32)
     p = mom_ref[...] - half * q
     total = x * y * c
-    drifts = []
     for k in range(steps):
         noise = noise_ref[k * total : (k + 1) * total].astype(jnp.float32)
         q = q + push * p + (half * kick) * noise
@@ -446,18 +479,30 @@
             flat = turn(loose.at[k], at).astype(jnp.bfloat16)
             for r in range(ring):
                 msgd[k, r, at] = flat[r * zb : (r + 1) * zb]
-        gotd[k, me] = msgd[k, me]
     fixed[0] = q
     fixed[1] = p
 
     def send_drift(k):
-        drifts.append(to_ring(lambda r: msgd.at[k, r], gotd.at[k, me]))
-
-    other = {"gz": (iz + 1) % nz}
-    pass_on(head, column_a, across_a)
-    pass_on(tail, column_b, across_b)
-    arrive(across_a)
-    swap_a = start(all_w.at[:, head], all_w.at[:, head], other)
+        to_owners(msgd.at[k], gotd.at[k, me], drift_sem[k])
+
+    @pl.when(outer)
+    def _():
+        pass_on(0)
+        pass_on(1)
+
+    send_drift(0)
+
+    def swap(which):
+        @pl.when(outer)
+        def _():
+            arrive(across_sem[which], all_w.at[which, 0:nx])
+            start(all_w.at[which], all_w.at[which], swap_sem[which], other)
+
+    def swapped(which):
+        @pl.when(jnp.logical_not(outer))
+        def _():
+            arrive(swap_sem[which], all_w.at[which])
+
     at_lane = lax.broadcasted_iota(jnp.int32, (co, lane), 1)
 
     def build(which):
@@ -468,12 +513,12 @@
                     moved = {}
                     for b in range(3):
                         t = a * 9 + b * 3 + cz
-                        tile, spot = which * tiles + t // per, t % per
+                        tile, spot = t // per, t % per
                         for side in range(2):
                             pieces = []
                             for gy in range(ny):
                                 r = gy * nx + gx + (gy % 2) * (nx - 1 - 2 * gx)
-                                piece = all_w[r, tile].astype(jnp.float32)
+                                piece = all_w[which, r, tile].astype(jnp.float32)
                                 shift = (side * ny + gy - spot) % per
                                 pieces.append(pltpu.roll(piece, shift * ci, 1) if shift else piece)
                             moved[b, side] = pieces
@@ -509,13 +554,13 @@
     def whole(ref, rows_from, rows_to):
         return jnp.concatenate([ref[gy, rows_from:rows_to] for gy in range(ny)], axis=1)
 
-    arrive([swap_a])
+    swap(0)
+    swapped(0)
     build(0)
-    arrive(across_b)
-    swap_b = start(all_w.at[:, tail], all_w.at[:, tail], other)
+    swap(1)
     turn_over(0)
-    arrive(fields)
-    send_drift(0)
+    arrive(field_sem, got0)
+    send_drift(1)
     for r in range(ring):
         around = got0[r, x].astype(jnp.float32)
         for at in range(x):
@@ -576,15 +621,14 @@
         return conv(3, 0, True)
 
     def take_drift(k):
-        arrive(drifts[k])
+        arrive(drift_sem[k], gotd.at[k])
         for r in range(ring):
             for at in range(x):
                 scatter(extra, 0, gotd[k, r, at].astype(jnp.float32), r, at)
         base[...] = base[...] + whole(extra, 0, rows)
 
     def second_filters():
-        arrive([swap_b])
-        send_drift(1)
+        swapped(1)
         build(1)
 
     def collect(ref, r, at):
@@ -603,16 +647,15 @@
     put(dq, (-half * push) * g)
     take_drift(0)
 
-    left_r, right_r = (me + ring - 1) % ring, (me + 1) % ring
-    left = device(left_r, (iz + nz - 1 + (me + ring - 1) // ring) % nz)
-    right = device(right_r, (iz + (me + 1) // ring) % nz)
+    left = device((me + ring - 1 + iz) % ring, 1 - iz)
+    right = device((me + iz) % ring, 1 - iz)
     edge = reach * xx
-    mine = pl.ds(pl.multiple_of(me * zb, zb), zb)
+    mine = pl.ds(pl.multiple_of(filed * zb, zb), zb)
     for k in range(1, steps + 1):
         q = base[...] + whole(dq, 0, rows)
         qb[k - 1] = q.astype(jnp.bfloat16)
-        below = start(qb.at[k - 1, rows - edge : rows], halo.at[k - 1, 0], right)
-        above = start(qb.at[k - 1, 0:edge], halo.at[k - 1, 1], left)
+        start(qb.at[k - 1, rows - edge : rows], halo.at[k - 1, 0], halo_sem[k - 1], right)
+        start(qb.at[k - 1, 0:edge], halo.at[k - 1, 1], halo_sem[k - 1], left)
         if k == 1:
             for later in range(2, steps):
                 send_drift(later)
@@ -623,14 +666,12 @@
             dp[...] = decay * dp[...] - half * dq[...]
             for r in range(ring):
                 for at in range(x):
-                    back_q[r, at] = collect(dq, r, at)
+                    back_q[r, at] = collect(dq, r, at).astype(jnp.bfloat16)
                     back_p[0, r, at] = collect(dp, r, at).astype(jnp.bfloat16)
-            sent_q = to_ring(lambda r: back_q.at[r], got_q.at[:, mine])
-            sent_p = to_ring(lambda r: back_p.at[0, r], got_p.at[0, :, mine])
-            got_q[:, mine] = back_q[me]
-            got_p[0, :, mine] = back_p[0, me]
+            to_sources(back_q, got_q.at[:, mine], q_sem)
+            to_sources(back_p.at[0], got_p.at[0, :, mine], p_sem[0])
             dp[...] = dp[...] - dp[...].astype(jnp.bfloat16).astype(jnp.float32)
-        arrive([below, above])
+        arrive(halo_sem[k - 1], halo.at[k - 1])
         spread(
             jnp.concatenate(
                 [halo[k - 1, 0].astype(jnp.float32), q, halo[k - 1, 1].astype(jnp.float32)], axis=0
@@ -647,8 +688,7 @@
     for r in range(ring):
         for at in range(x):
             back_p[1, r, at] = collect(dp, r, at).astype(jnp.bfloat16)
-    last_p = to_ring(lambda r: back_p.at[1, r], got_p.at[1, :, mine])
-    got_p[1, :, mine] = back_p[1, me]
+    to_sources(back_p.at[1], got_p.at[1, :, mine], p_sem[1])
 
     def untie(value, which, out, at):
         flat = value.T
@@ -656,15 +696,30 @@
             part = pl.ds(at * y + j, c, stride=x * y)
             out[part, :] = fixed[which, part, :] + flat[j * c : (j + 1) * c]
 
-    arrive(sent_q)
+    arrive(q_sem, got_q)
     for at in range(x):
-        untie(got_q[at], 0, q_out, at)
-    arrive(sent_p)
-    arrive(last_p)
+        untie(got_q[at].astype(jnp.float32), 0, q_out, at)
+    arrive(p_sem[0], got_p.at[0])
+    arrive(p_sem[1], got_p.at[1])
     for at in range(x):
         untie(got_p[0, at].astype(jnp.float32) + got_p[1, at].astype(jnp.float32), 1, p_out, at)
-    for copy in sent:
-        copy.wait_send()
+
+    @pl.when(outer)
+    def _():
+        for which in range(2):
+            for number in column_sems[which]:
+                leave(number, own_w.at[which])
+            leave(across_sem[which], all_w.at[which, 0:nx])
+            leave(swap_sem[which], all_w.at[which])
+
+    leave(edge_sem, edges)
+    left_ring(field_sem, msg0)
+    for k in range(steps):
+        left_ring(drift_sem[k], msgd.at[k])
+        leave(halo_sem[k], halo.at[k])
+    left_ring(q_sem, back_q)
+    for part in range(2):
+        left_ring(p_sem[part], back_p.at[part])
 
 
 def fits_ring(sizes, position, filter_in):
@@ -692,7 +747,7 @@
     lane = LANES
     tiles = -(-27 * ci // lane)
     flat = jax.ShapeDtypeStruct((c * x * y, z), jnp.float32)
-    copies = (4 + steps) * (ring - 1) + 4 * nx + 4 + 2 * steps
+    copies = 2 * nx + 7 + 2 * steps
     heights = [(zb + 2 * reach) * xx for reach in (3, 2, 1, 0)]
     vmem = pl.BlockSpec(memory_space=pltpu.VMEM)
     bf16, f32 = jnp.bfloat16, jnp.float32
@@ -708,8 +763,8 @@
             pltpu.VMEM((27, co, ci), bf16),
             pltpu.VMEM((27, co, ci), bf16),
             pltpu.VMEM((1, c), f32),
-            pltpu.VMEM((2 * tiles, co, lane), bf16),
-            pltpu.VMEM((ring, 2 * tiles, co, lane), bf16),
+            pltpu.VMEM((2, tiles, co, lane), bf16),
+            pltpu.VMEM((2, ring, tiles, co, lane), bf16),
             pltpu.VMEM((2, 9, wide, wide), bf16),
             pltpu.VMEM((2, 9, wide, wide), bf16),
             pltpu.VMEM((x, z, lane), f32),
@@ -727,8 +782,8 @@
             pltpu.VMEM((ny, rows, lane), f32),
             pltpu.VMEM((steps, rows, wide), bf16),
             pltpu.VMEM((steps, 2, 4 * xx, wide), bf16),
-            pltpu.VMEM((ring, x, zb, lane), f32),
-            pltpu.VMEM((x, z, lane), f32),
+            pltpu.VMEM((ring, x, zb, lane), bf16),
+            pltpu.VMEM((x, z, lane), bf16),
             pltpu.VMEM((2, ring, x, zb, lane), bf16),
             pltpu.VMEM((2, x, z, lane), bf16),
             pltpu.VMEM((2, c * x * y, z), f32),

time: 39.4 us -> 34.3 us (0.87)
  Pallas kernels: 37.3 us -> 32 us
    pallas_call x1, Pallas kernels: 37.3 us -> 32 us  [on_ring(): pl.pallas_call(functools.partial(ring_kernel, steps, sizes, heights), out...]
where the time goes in v3:
time: 34.3 us; the launch traced here: 34 us
  Pallas kernels  32 us (93%)
  local copies, waits for them, and re-layouts  1.31 us (4%)
  between operations  0.64 us (2%)
    pallas_call x1, Pallas kernels, on_ring(): pl.pallas_call(functools.partial(ring_kernel, steps, sizes, heights), out...  32 us
    unnamed x2, local copies, waits for them, and re-layouts  1.31 us

profile of v3, /device:TPU:0, one launch (start us, length us, event | category | flops | bytes accessed | tf_op | source)
XLA Modules:
  0.0 34.0 jit_solution(7442056432153237339)
XLA Ops:
  0.6 32.0 %shard_map.77 = (f32[256,128]{1,0:T(8,128)S(1)}, f32[256,128]{1,0:T(8,128)S(1)}) custom-call(f32[256,128]{1,0:T(8,128)} %bitcast.15, f32[256,128]{1,0:T(8,128)} %bitcast.16, bf16[768,128]{1,0:T(8,128)(2,1)} %bitcast.14, bf16[27,16,32]{2,1,0:T(8,128)(2,1)} %bitcast.17, bf16[27,16,32]{2,1,0:T(8,128)(2,1)} %bitcast.18, f32[1,64]{1,0:T(1,128)} %bitcast.19), custom_call_target="tpu_custom_call" | custom-call | tf_op jit(solution)/shard_map/pallas_call | solution.py:754
  32.6 0.7 %copy.10 = f32[64,2,2,128]{3,2,1,0:T(2,128)} copy(f32[64,2,2,128]{3,2,1,0:T(2,128)S(1)} %bitcast.13) | data formatting | bytes 262144
  33.3 0.7 %copy.11 = f32[64,2,2,128]{3,2,1,0:T(2,128)} copy(f32[64,2,2,128]{3,2,1,0:T(2,128)S(1)} %bitcast.12) | data formatting | bytes 262144

commit v4 on v3

--- a/solution.py
+++ b/solution.py
@@ -266,29 +266,32 @@
     return step + (row % 2) * (nx - 1 - 2 * step), row
 
 
+def split_rows(height):
+    low = -(-height // (2 * EDGE)) * EDGE
+    return low, height - low
+
+
 def ring_kernel(steps, sizes, heights, *refs):
-    accs = []
-    for unit in range(2):
-        for height in heights:
-            low = -(-height // (2 * EDGE)) * EDGE
-            for part in (low, height - low):
-                accs.append(pltpu.ACC(unit)((part, 2 * LANES), jnp.float32))
-    pl.run_scoped(functools.partial(ring_body, steps, sizes, refs), *accs)
-
-
-def ring_body(steps, sizes, refs, *sums):
+    pool = {}
+    for height in heights:
+        parts = split_rows(height)
+        for part in parts:
+            pool[part] = max(pool.get(part, 0), parts.count(part))
+    order = [(unit, part, i) for unit in range(2) for part in sorted(pool) for i in range(pool[part])]
+    spaces = [pltpu.ACC(unit)((part, 2 * LANES), jnp.float32) for unit, part, _ in order]
+    pl.run_scoped(functools.partial(ring_body, steps, sizes, order, refs), *spaces)
+
+
+def ring_body(steps, sizes, order, refs, *sums):
     nx, ny, nz = sizes
-    count = len(sums) // 2
-    accs = [
-        [[sums[unit * count + 2 * place + part] for part in range(2)] for unit in range(2)]
-        for place in range(count // 2)
-    ]
+    banks = dict(zip(order, sums))
     inputs, refs = refs[:6], refs[6:]
     (q_out, p_out, pos_ref, mom_ref, noise_ref, fin_ref, fout_ref, bias_ref, own_w, all_w, mats,
-     flipped, turned, edges, msg0, got0, msgd, gotd, stage, lhs, t_ref, base, extra, dq, dp, qb,
-     halo, back_q, got_q, back_p, got_p, fixed, loose, send, recv, load) = refs
+     flipped, turned, turned_d, edges, msg0, got0, msgd, gotd, stage, lhs, t_ref, base, extra, dq, dp, qb,
+     halo, vb, ring_v, back_q, got_q, back_p, got_p, fixed, loose, edges_d, msge, gote, send, recv,
+     load) = refs
     ring = nx * ny
-    x, zb = msg0.shape[1] - 1, msg0.shape[2]
+    x, zb = msg0.shape[1] // 2, msg0.shape[2]
     lane = LANES
     z = ring * zb
     taps, co, ci = fin_ref.shape
@@ -390,8 +393,12 @@
     swap_sem = [2 * nx, 2 * nx + 1]
     edge_sem, field_sem = 2 * nx + 2, 2 * nx + 3
     drift_sem = [2 * nx + 4 + k for k in range(steps)]
-    halo_sem = [2 * nx + 4 + steps + k for k in range(steps)]
-    q_sem, p_sem = 2 * nx + 4 + 2 * steps, [2 * nx + 5 + 2 * steps, 2 * nx + 6 + 2 * steps]
+    pairs = (steps - 1) // 2
+    q_sem = 2 * nx + 4 + steps
+    p_sem = [q_sem + 1, q_sem + 2]
+    drift_edge_sem = q_sem + 3
+    halo_sem = [q_sem + 4 + k for k in range(pairs)]
+    v_sem = [q_sem + 4 + pairs + k for k in range(pairs)]
 
     outer = iz == nz - 1
     loads[0].wait()
@@ -445,15 +452,18 @@
         all_w[:, me] = own_w[...]
 
     upper = lax.broadcasted_iota(jnp.int32, (ROWS, lane), 0) < reach
+
+    def around(ref, beyond, r, at):
+        before = ref[at, r * zb - ROWS : r * zb] if r else beyond[0, at]
+        after = ref[at, (r + 1) * zb : (r + 1) * zb + ROWS] if r < ring - 1 else beyond[1, at]
+        return before, after
+
     arrive(edge_sem, edges)
     for r in range(ring):
-        around = []
         for at in range(x):
             msg0[r, at] = turned[at, r * zb : (r + 1) * zb].astype(jnp.bfloat16)
-            before = turned[at, r * zb - ROWS : r * zb] if r else edges[0, at]
-            after = turned[at, (r + 1) * zb : (r + 1) * zb + ROWS] if r < ring - 1 else edges[1, at]
-            around.append(jnp.where(upper, after, before))
-        msg0[r, x] = jnp.concatenate(around, axis=0).astype(jnp.bfloat16)
+            before, after = around(turned, edges, r, at)
+            msg0[r, x + at] = jnp.concatenate([after, before], axis=0).astype(jnp.bfloat16)
     to_owners(msg0, got0.at[me], field_sem)
 
     half = 0.125
@@ -476,27 +486,51 @@
         p = decay * p + kick * noise - (half if last else 2 * half) * q
         loose[k] = drift
         for at in range(x):
-            flat = turn(loose.at[k], at).astype(jnp.bfloat16)
-            for r in range(ring):
-                msgd[k, r, at] = flat[r * zb : (r + 1) * zb]
+            flat = turn(loose.at[k], at)
+            if k == 0:
+                turned_d[at] = flat
+                for r in range(ring):
+                    msge[r, at] = flat[r * zb : (r + 1) * zb].astype(jnp.bfloat16)
+            else:
+                flat = flat.astype(jnp.bfloat16)
+                for r in range(ring):
+                    msgd[k - 1, r, at] = flat[r * zb : (r + 1) * zb]
+        if k == 0:
+            start(turned_d.at[:, z - ROWS : z], edges_d.at[0], drift_edge_sem, {"gz": (iz + 1) % nz})
+            start(turned_d.at[:, 0:ROWS], edges_d.at[1], drift_edge_sem, {"gz": (iz + nz - 1) % nz})
     fixed[0] = q
     fixed[1] = p
 
     def send_drift(k):
-        to_owners(msgd.at[k], gotd.at[k, me], drift_sem[k])
+        if k == 0:
+            to_owners(msge, gote.at[me], drift_sem[0])
+        else:
+            to_owners(msgd.at[k - 1], gotd.at[k - 1, me], drift_sem[k])
 
     @pl.when(outer)
     def _():
         pass_on(0)
+
+    arrive(drift_edge_sem, edges_d)
+    for r in range(ring):
+        beyond = []
+        for at in range(x):
+            before, after = around(turned_d, edges_d, r, at)
+            beyond.append(jnp.where(upper, after, before))
+        msge[r, x] = jnp.concatenate(beyond, axis=0).astype(jnp.bfloat16)
+    send_drift(0)
+
+    def swap(which):
+        arrive(across_sem[which], all_w.at[which, 0:nx])
+        start(all_w.at[which], all_w.at[which], swap_sem[which], other)
+
+    @pl.when(outer)
+    def _():
+        swap(0)
         pass_on(1)
 
-    send_drift(0)
-
-    def swap(which):
-        @pl.when(outer)
-        def _():
-            arrive(across_sem[which], all_w.at[which, 0:nx])
-            start(all_w.at[which], all_w.at[which], swap_sem[which], other)
+    for later in range(1, steps):
+        send_drift(later)
 
     def swapped(which):
         @pl.when(jnp.logical_not(outer))
@@ -554,19 +588,19 @@
     def whole(ref, rows_from, rows_to):
         return jnp.concatenate([ref[gy, rows_from:rows_to] for gy in range(ny)], axis=1)
 
-    swap(0)
     swapped(0)
     build(0)
-    swap(1)
+
+    @pl.when(outer)
+    def _():
+        swap(1)
+
     turn_over(0)
     arrive(field_sem, got0)
-    send_drift(1)
     for r in range(ring):
-        around = got0[r, x].astype(jnp.float32)
         for at in range(x):
             scatter(stage, 0, got0[r, at].astype(jnp.float32), r, at)
-            scatter(stage, zb, around[at * ROWS : (at + 1) * ROWS], r, at)
-    base[...] = whole(stage, 0, rows)
+            scatter(stage, zb, got0[r, x + at].astype(jnp.float32), r, at)
 
     def spread(value):
         n = value.shape[0]
@@ -577,10 +611,10 @@
             lhs[a, 0, 0:n] = moved.astype(jnp.bfloat16)
             lhs[a, 1, 0 : n - 2 * xx] = moved[xx : n - xx].astype(jnp.bfloat16)
 
-    def conv(place, which, adjoint, flip=False):
+    def conv(height, which, adjoint, flip=False):
         source = mats if adjoint or flip else flipped
-        sums = accs[place]
-        low, high = sums[0][0].shape[0], sums[0][1].shape[0]
+        low, high = split_rows(height)
+        sums = [[banks[unit, low, 0], banks[unit, high, int(low == high)]] for unit in range(2)]
         plans = (
             [(0, True, True), (1, True, True), (2, True, True), (3, True, True), (4, True, False)],
             [(8, True, True), (7, True, True), (6, True, True), (5, True, True), (4, False, True)],
@@ -609,22 +643,23 @@
 
     row = jnp.concatenate([bias_ref[...]] * yy, axis=1)
 
-    def gradient(between, flip=False):
-        t = jnp.tanh(conv(0, 0, False) + row)
-        t_ref[...] = t
+    def gradient(extent, between=lambda: None, flip=False):
+        n = [rows + 2 * (extent + 3 - i) * xx for i in range(4)]
+        t = jnp.tanh(conv(n[0], 0, False) + row)
+        t_ref[0 : n[0]] = t
         spread(t)
         between()
-        spread(conv(1, 1, False, flip))
-        gu = conv(2, 1, True)
-        t = t_ref[2 * xx : 2 * xx + gu.shape[0]]
+        spread(conv(n[1], 1, False, flip))
+        gu = conv(n[2], 1, True)
+        t = t_ref[2 * xx : 2 * xx + n[2]]
         spread(gu * (1.0 - t * t))
-        return conv(3, 0, True)
+        return conv(n[3], 0, True)
 
     def take_drift(k):
-        arrive(drift_sem[k], gotd.at[k])
+        arrive(drift_sem[k], gotd.at[k - 1])
         for r in range(ring):
             for at in range(x):
-                scatter(extra, 0, gotd[k, r, at].astype(jnp.float32), r, at)
+                scatter(extra, 0, gotd[k - 1, r, at].astype(jnp.float32), r, at)
         base[...] = base[...] + whole(extra, 0, rows)
 
     def second_filters():
@@ -639,52 +674,77 @@
         for gy in range(ny):
             ref[gy] = value[:, gy * lane : (gy + 1) * lane]
 
-    turn_at = (zb + reach) * xx
-    field = [whole(stage, turn_at, turn_at + reach * xx), whole(stage, 0, turn_at)]
-    spread(jnp.concatenate(field, axis=0))
-    g = gradient(second_filters, True)
-    put(dp, -half * g)
-    put(dq, (-half * push) * g)
-    take_drift(0)
+    edge = reach * xx
+    full = rows + 4 * edge
+    ends = [whole(stage, full - 2 * edge, full), whole(stage, 0, full - 2 * edge)]
+    spread(jnp.concatenate(ends, axis=0))
+    g = gradient(reach, second_filters, True)
+
+    arrive(drift_sem[0], gote)
+    for r in range(ring):
+        beyond = gote[r, x].astype(jnp.float32)
+        for at in range(x):
+            scatter(extra, 0, gote[r, at].astype(jnp.float32), r, at)
+            scatter(extra, zb, beyond[at * ROWS : (at + 1) * ROWS], r, at)
+    now = whole(stage, 0, rows) + whole(extra, 0, rows)
+    base[...] = now
+    above = whole(stage, rows, rows + edge) + whole(extra, rows, rows + edge)
+    below = whole(stage, full - edge, full) + whole(extra, rows + edge, rows + 2 * edge)
+    force = g[edge : edge + rows]
+    put(dp, -half * force)
+    put(dq, (-half * push) * force)
+    spread(jnp.concatenate([below, now, above], axis=0) + (-half * push) * g)
 
     left = device((me + ring - 1 + iz) % ring, 1 - iz)
     right = device((me + iz) % ring, 1 - iz)
-    edge = reach * xx
     mine = pl.ds(pl.multiple_of(filed * zb, zb), zb)
-    for k in range(1, steps + 1):
+
+    def kicked(g):
+        shift = whole(dq, 0, rows)
+        now = decay * whole(dp, 0, rows) - (2 * half) * (g + shift)
+        put(dp, now)
+        put(dq, shift + push * now)
+
+    for pair in range(pairs):
+        kicked(gradient(0, flip=pair == 0))
+        k = 2 * pair + 2
+        take_drift(k - 1)
         q = base[...] + whole(dq, 0, rows)
-        qb[k - 1] = q.astype(jnp.bfloat16)
-        start(qb.at[k - 1, rows - edge : rows], halo.at[k - 1, 0], halo_sem[k - 1], right)
-        start(qb.at[k - 1, 0:edge], halo.at[k - 1, 1], halo_sem[k - 1], left)
-        if k == 1:
-            for later in range(2, steps):
-                send_drift(later)
+        qb[pair] = q.astype(jnp.bfloat16)
+        start(qb.at[pair, rows - 2 * edge : rows], halo.at[pair, 0], halo_sem[pair], right)
+        start(qb.at[pair, 0 : 2 * edge], halo.at[pair, 1], halo_sem[pair], left)
+        if pair == 0:
             turn_over(1)
-        if k < steps:
-            take_drift(k)
-        else:
-            dp[...] = decay * dp[...] - half * dq[...]
-            for r in range(ring):
-                for at in range(x):
-                    back_q[r, at] = collect(dq, r, at).astype(jnp.bfloat16)
-                    back_p[0, r, at] = collect(dp, r, at).astype(jnp.bfloat16)
-            to_sources(back_q, got_q.at[:, mine], q_sem)
-            to_sources(back_p.at[0], got_p.at[0, :, mine], p_sem[0])
-            dp[...] = dp[...] - dp[...].astype(jnp.bfloat16).astype(jnp.float32)
-        arrive(halo_sem[k - 1], halo.at[k - 1])
-        spread(
-            jnp.concatenate(
-                [halo[k - 1, 0].astype(jnp.float32), q, halo[k - 1, 1].astype(jnp.float32)], axis=0
-            )
-        )
-        g = gradient(lambda: None)
-        if k < steps:
-            shift = whole(dq, 0, rows)
-            now = decay * whole(dp, 0, rows) - (2 * half) * (g + shift)
-            put(dp, now)
-            put(dq, shift + push * now)
-        else:
-            put(dp, whole(dp, 0, rows) - half * g)
+        take_drift(k)
+        shift = whole(dq, 0, rows)
+        v = base[...] + shift + push * (decay * whole(dp, 0, rows) - (2 * half) * shift)
+        vb[pair] = v.astype(jnp.bfloat16)
+        start(vb.at[pair, rows - edge : rows], ring_v.at[pair, 0], v_sem[pair], right)
+        start(vb.at[pair, 0:edge], ring_v.at[pair, 1], v_sem[pair], left)
+        arrive(halo_sem[pair], halo.at[pair])
+        ends = [halo[pair, side].astype(jnp.float32) for side in range(2)]
+        spread(jnp.concatenate([ends[0], q, ends[1]], axis=0))
+        g = gradient(reach)
+        kicked(g[edge : edge + rows])
+        q = base[...] + whole(dq, 0, rows)
+        arrive(v_sem[pair], ring_v.at[pair])
+        ends = [
+            ring_v[pair, side].astype(jnp.float32) - (2 * half * push) * g[at : at + edge]
+            for side, at in enumerate((0, edge + rows))
+        ]
+        spread(jnp.concatenate([ends[0], q, ends[1]], axis=0))
+
+    put(dp, decay * whole(dp, 0, rows) - half * whole(dq, 0, rows))
+    for r in range(ring):
+        for at in range(x):
+            back_q[r, at] = collect(dq, r, at).astype(jnp.bfloat16)
+            back_p[0, r, at] = collect(dp, r, at).astype(jnp.bfloat16)
+    to_sources(back_q, got_q.at[:, mine], q_sem)
+    to_sources(back_p.at[0], got_p.at[0, :, mine], p_sem[0])
+    g = gradient(0)
+    left_over = whole(dp, 0, rows)
+    left_over = left_over - left_over.astype(jnp.bfloat16).astype(jnp.float32)
+    put(dp, left_over - half * g)
     for r in range(ring):
         for at in range(x):
             back_p[1, r, at] = collect(dp, r, at).astype(jnp.bfloat16)
@@ -713,22 +773,26 @@
             leave(swap_sem[which], all_w.at[which])
 
     leave(edge_sem, edges)
+    leave(drift_edge_sem, edges_d)
     left_ring(field_sem, msg0)
-    for k in range(steps):
-        left_ring(drift_sem[k], msgd.at[k])
-        leave(halo_sem[k], halo.at[k])
+    left_ring(drift_sem[0], msge)
+    for k in range(1, steps):
+        left_ring(drift_sem[k], msgd.at[k - 1])
+    for pair in range(pairs):
+        leave(halo_sem[pair], halo.at[pair])
+        leave(v_sem[pair], ring_v.at[pair])
     left_ring(q_sem, back_q)
     for part in range(2):
         left_ring(p_sem[part], back_p.at[part])
 
 
-def fits_ring(sizes, position, filter_in):
+def fits_ring(steps, sizes, position, filter_in):
     nx, ny, nz = sizes
     c, x, y, z = position.shape
     co, ci = filter_in.shape[:2]
     ring = nx * ny
     return (
-        nz == 2 and ny == 2 and nx > 1 and y * c == LANES and x * nx == ROWS and y * ny > 2
+        steps % 2 == 1 and steps > 2 and nz == 2 and ny == 2 and nx > 1 and y * c == LANES and x * nx == ROWS and y * ny > 2
         and z % (ring * EDGE) == 0 and z // ring == EDGE and co % EDGE == 0 and LANES % ci == 0
         and y * ny * ci == LANES
     )
@@ -747,8 +811,10 @@
     lane = LANES
     tiles = -(-27 * ci // lane)
     flat = jax.ShapeDtypeStruct((c * x * y, z), jnp.float32)
-    copies = 2 * nx + 7 + 2 * steps
-    heights = [(zb + 2 * reach) * xx for reach in (3, 2, 1, 0)]
+    reach, pairs = 4, (steps - 1) // 2
+    copies = 2 * nx + 8 + steps + 2 * pairs
+    edge = reach * xx
+    heights = [(zb + 2 * beyond) * xx for beyond in range(2 * reach)]
     vmem = pl.BlockSpec(memory_space=pltpu.VMEM)
     bf16, f32 = jnp.bfloat16, jnp.float32
     q, p = pl.pallas_call(
@@ -768,26 +834,32 @@
             pltpu.VMEM((2, 9, wide, wide), bf16),
             pltpu.VMEM((2, 9, wide, wide), bf16),
             pltpu.VMEM((x, z, lane), f32),
+            pltpu.VMEM((x, z, lane), f32),
             pltpu.VMEM((2, x, ROWS, lane), f32),
-            pltpu.VMEM((ring, x + 1, zb, lane), bf16),
-            pltpu.VMEM((ring, x + 1, zb, lane), bf16),
-            pltpu.VMEM((steps, ring, x, zb, lane), bf16),
-            pltpu.VMEM((steps, ring, x, zb, lane), bf16),
-            pltpu.VMEM((ny, rows + ROWS * xx, lane), f32),
-            pltpu.VMEM((3, 2, rows + ROWS * xx, wide), bf16),
-            pltpu.VMEM((rows + 6 * xx, wide), f32),
+            pltpu.VMEM((ring, 2 * x, zb, lane), bf16),
+            pltpu.VMEM((ring, 2 * x, zb, lane), bf16),
+            pltpu.VMEM((steps - 1, ring, x, zb, lane), bf16),
+            pltpu.VMEM((steps - 1, ring, x, zb, lane), bf16),
+            pltpu.VMEM((ny, rows + 4 * edge, lane), f32),
+            pltpu.VMEM((3, 2, rows + 4 * edge, wide), bf16),
+            pltpu.VMEM((rows + 4 * edge - 2 * xx, wide), f32),
             pltpu.VMEM((rows, wide), f32),
+            pltpu.VMEM((ny, rows + 2 * edge, lane), f32),
             pltpu.VMEM((ny, rows, lane), f32),
             pltpu.VMEM((ny, rows, lane), f32),
-            pltpu.VMEM((ny, rows, lane), f32),
-            pltpu.VMEM((steps, rows, wide), bf16),
-            pltpu.VMEM((steps, 2, 4 * xx, wide), bf16),
+            pltpu.VMEM((pairs, rows, wide), bf16),
+            pltpu.VMEM((pairs, 2, 2 * edge, wide), bf16),
+            pltpu.VMEM((pairs, rows, wide), bf16),
+            pltpu.VMEM((pairs, 2, edge, wide), bf16),
             pltpu.VMEM((ring, x, zb, lane), bf16),
             pltpu.VMEM((x, z, lane), bf16),
             pltpu.VMEM((2, ring, x, zb, lane), bf16),
             pltpu.VMEM((2, x, z, lane), bf16),
             pltpu.VMEM((2, c * x * y, z), f32),
             pltpu.VMEM((steps, c * x * y, z), f32),
+            pltpu.VMEM((2, x, ROWS, lane), f32),
+            pltpu.VMEM((ring, x + 1, zb, lane), bf16),
+            pltpu.VMEM((ring, x + 1, zb, lane), bf16),
             pltpu.SemaphoreType.DMA((copies,)),
             pltpu.SemaphoreType.DMA((copies,)),
             pltpu.SemaphoreType.DMA((6,)),
@@ -812,7 +884,7 @@
 
 
 def on_device(sizes, position, momentum, noise, filter_in, filter_out, bias):
-    if fits_ring(sizes, position, filter_in):
+    if fits_ring(noise.shape[0], sizes, position, filter_in):
         return on_ring(sizes, position, momentum, noise, filter_in, filter_out, bias)
     nx, ny, nz = sizes
     c, x, y, z = position.shape

time: 34.3 us -> 33.5 us (0.977)
  Pallas kernels: 32 us -> 31.4 us
    pallas_call x1, Pallas kernels: 32 us -> 31.4 us  [on_ring(): pl.pallas_call(functools.partial(ring_kernel, steps, sizes, heights), out...]
where the time goes in v4:
time: 33.5 us; the launch traced here: 33.3 us
  Pallas kernels  31.4 us (94%)
  local copies, waits for them, and re-layouts  1.31 us (4%)
  between operations  0.64 us (2%)
    pallas_call x1, Pallas kernels, on_ring(): pl.pallas_call(functools.partial(ring_kernel, steps, sizes, heights), out...  31.4 us
    unnamed x2, local copies, waits for them, and re-layouts  1.31 us

profile of v4, /device:TPU:0, one launch (start us, length us, event | category | flops | bytes accessed | tf_op | source)
XLA Modules:
  0.0 33.3 jit_solution(11338537822106064672)
XLA Ops:
  0.6 31.4 %shard_map.77 = (f32[256,128]{1,0:T(8,128)S(1)}, f32[256,128]{1,0:T(8,128)S(1)}) custom-call(f32[256,128]{1,0:T(8,128)} %bitcast.15, f32[256,128]{1,0:T(8,128)} %bitcast.16, bf16[768,128]{1,0:T(8,128)(2,1)} %bitcast.14, bf16[27,16,32]{2,1,0:T(8,128)(2,1)} %bitcast.17, bf16[27,16,32]{2,1,0:T(8,128)(2,1)} %bitcast.18, f32[1,64]{1,0:T(1,128)} %bitcast.19), custom_call_target="tpu_custom_call" | custom-call | tf_op jit(solution)/shard_map/pallas_call | solution.py:820
  32.0 0.7 %copy.10 = f32[64,2,2,128]{3,2,1,0:T(2,128)} copy(f32[64,2,2,128]{3,2,1,0:T(2,128)S(1)} %bitcast.13) | data formatting | bytes 262144
  32.7 0.7 %copy.11 = f32[64,2,2,128]{3,2,1,0:T(2,128)} copy(f32[64,2,2,128]{3,2,1,0:T(2,128)S(1)} %bitcast.12) | data formatting | bytes 262144

commit v5 on v4

--- a/solution.py
+++ b/solution.py
@@ -287,11 +287,11 @@
     banks = dict(zip(order, sums))
     inputs, refs = refs[:6], refs[6:]
     (q_out, p_out, pos_ref, mom_ref, noise_ref, fin_ref, fout_ref, bias_ref, own_w, all_w, mats,
-     flipped, turned, turned_d, edges, msg0, got0, msgd, gotd, stage, lhs, t_ref, base, extra, dq, dp, qb,
+     flipped, turned_d, msg0, got0, msgd, gotd, stage, lhs, t_ref, base, extra, dq, dp, qb,
      halo, vb, ring_v, back_q, got_q, back_p, got_p, fixed, loose, edges_d, msge, gote, send, recv,
      load) = refs
     ring = nx * ny
-    x, zb = msg0.shape[1] // 2, msg0.shape[2]
+    x, zb = msg0.shape[1], msg0.shape[2]
     lane = LANES
     z = ring * zb
     taps, co, ci = fin_ref.shape
@@ -391,13 +391,12 @@
     column_sems = [[which * (nx - 1) + dx for dx in range(nx - 1)] for which in range(2)]
     across_sem = [2 * (nx - 1), 2 * (nx - 1) + 1]
     swap_sem = [2 * nx, 2 * nx + 1]
-    edge_sem, field_sem = 2 * nx + 2, 2 * nx + 3
-    drift_sem = [2 * nx + 4 + k for k in range(steps)]
+    field_sem = 2 * nx + 2
+    drift_sem = [2 * nx + 3 + k for k in range(steps)]
     pairs = (steps - 1) // 2
-    q_sem = 2 * nx + 4 + steps
-    p_sem = [q_sem + 1, q_sem + 2]
-    drift_edge_sem = q_sem + 3
-    halo_sem = [q_sem + 4 + k for k in range(pairs)]
+    q_sem = 2 * nx + 3 + steps
+    p_sem, drift_edge_sem = q_sem + 1, q_sem + 2
+    halo_sem = [q_sem + 3 + k for k in range(pairs + 1)]
     v_sem = [q_sem + 4 + pairs + k for k in range(pairs)]
 
     outer = iz == nz - 1
@@ -419,7 +418,9 @@
 
     loads[2].wait()
     for at in range(x):
-        turned[at] = turn(pos_ref, at)
+        flat = turn(pos_ref, at).astype(jnp.bfloat16)
+        for r in range(ring):
+            msg0[r, at] = flat[r * zb : (r + 1) * zb]
 
     for each in sums:
         pltpu.matmul_pop(each)
@@ -443,9 +444,6 @@
     def _():
         to_column(0)
 
-    start(turned.at[:, z - ROWS : z], edges.at[0], edge_sem, {"gz": (iz + 1) % nz})
-    start(turned.at[:, 0:ROWS], edges.at[1], edge_sem, {"gz": (iz + nz - 1) % nz})
-
     @pl.when(outer)
     def _():
         to_column(1)
@@ -458,12 +456,6 @@
         after = ref[at, (r + 1) * zb : (r + 1) * zb + ROWS] if r < ring - 1 else beyond[1, at]
         return before, after
 
-    arrive(edge_sem, edges)
-    for r in range(ring):
-        for at in range(x):
-            msg0[r, at] = turned[at, r * zb : (r + 1) * zb].astype(jnp.bfloat16)
-            before, after = around(turned, edges, r, at)
-            msg0[r, x + at] = jnp.concatenate([after, before], axis=0).astype(jnp.bfloat16)
     to_owners(msg0, got0.at[me], field_sem)
 
     half = 0.125
@@ -528,9 +520,6 @@
     def _():
         swap(0)
         pass_on(1)
-
-    for later in range(1, steps):
-        send_drift(later)
 
     def swapped(which):
         @pl.when(jnp.logical_not(outer))
@@ -588,19 +577,29 @@
     def whole(ref, rows_from, rows_to):
         return jnp.concatenate([ref[gy, rows_from:rows_to] for gy in range(ny)], axis=1)
 
-    swapped(0)
-    build(0)
-
-    @pl.when(outer)
-    def _():
-        swap(1)
-
-    turn_over(0)
+    left = device((me + ring - 1 + iz) % ring, 1 - iz)
+    right = device((me + iz) % ring, 1 - iz)
+    edge = reach * xx
+
+    def send_halo(slot, value):
+        qb[slot] = value.astype(jnp.bfloat16)
+        start(qb.at[slot, rows - 2 * edge : rows], halo.at[slot, 0], halo_sem[slot], right)
+        start(qb.at[slot, 0 : 2 * edge], halo.at[slot, 1], halo_sem[slot], left)
+
+    def with_halo(slot, value):
+        arrive(halo_sem[slot], halo.at[slot])
+        ends = [halo[slot, side].astype(jnp.float32) for side in range(2)]
+        return jnp.concatenate([ends[0], value, ends[1]], axis=0)
+
     arrive(field_sem, got0)
     for r in range(ring):
         for at in range(x):
             scatter(stage, 0, got0[r, at].astype(jnp.float32), r, at)
-            scatter(stage, zb, got0[r, x + at].astype(jnp.float32), r, at)
+    send_halo(0, whole(stage, 0, rows))
+    send_drift(1)
+    swapped(0)
+    build(0)
+    turn_over(0)
 
     def spread(value):
         n = value.shape[0]
@@ -663,7 +662,13 @@
         base[...] = base[...] + whole(extra, 0, rows)
 
     def second_filters():
+        @pl.when(outer)
+        def _():
+            swap(1)
+
         swapped(1)
+        for later in range(2, steps):
+            send_drift(later)
         build(1)
 
     def collect(ref, r, at):
@@ -674,10 +679,8 @@
         for gy in range(ny):
             ref[gy] = value[:, gy * lane : (gy + 1) * lane]
 
-    edge = reach * xx
-    full = rows + 4 * edge
-    ends = [whole(stage, full - 2 * edge, full), whole(stage, 0, full - 2 * edge)]
-    spread(jnp.concatenate(ends, axis=0))
+    base[...] = whole(stage, 0, rows)
+    spread(with_halo(0, base[...]))
     g = gradient(reach, second_filters, True)
 
     arrive(drift_sem[0], gote)
@@ -686,17 +689,15 @@
         for at in range(x):
             scatter(extra, 0, gote[r, at].astype(jnp.float32), r, at)
             scatter(extra, zb, beyond[at * ROWS : (at + 1) * ROWS], r, at)
-    now = whole(stage, 0, rows) + whole(extra, 0, rows)
+    now = base[...] + whole(extra, 0, rows)
     base[...] = now
-    above = whole(stage, rows, rows + edge) + whole(extra, rows, rows + edge)
-    below = whole(stage, full - edge, full) + whole(extra, rows + edge, rows + 2 * edge)
+    below = halo[0, 0, edge : 2 * edge].astype(jnp.float32) + whole(extra, rows + edge, rows + 2 * edge)
+    above = halo[0, 1, 0:edge].astype(jnp.float32) + whole(extra, rows, rows + edge)
     force = g[edge : edge + rows]
     put(dp, -half * force)
     put(dq, (-half * push) * force)
     spread(jnp.concatenate([below, now, above], axis=0) + (-half * push) * g)
 
-    left = device((me + ring - 1 + iz) % ring, 1 - iz)
-    right = device((me + iz) % ring, 1 - iz)
     mine = pl.ds(pl.multiple_of(filed * zb, zb), zb)
 
     def kicked(g):
@@ -710,9 +711,7 @@
         k = 2 * pair + 2
         take_drift(k - 1)
         q = base[...] + whole(dq, 0, rows)
-        qb[pair] = q.astype(jnp.bfloat16)
-        start(qb.at[pair, rows - 2 * edge : rows], halo.at[pair, 0], halo_sem[pair], right)
-        start(qb.at[pair, 0 : 2 * edge], halo.at[pair, 1], halo_sem[pair], left)
+        send_halo(pair + 1, q)
         if pair == 0:
             turn_over(1)
         take_drift(k)
@@ -721,9 +720,7 @@
         vb[pair] = v.astype(jnp.bfloat16)
         start(vb.at[pair, rows - edge : rows], ring_v.at[pair, 0], v_sem[pair], right)
         start(vb.at[pair, 0:edge], ring_v.at[pair, 1], v_sem[pair], left)
-        arrive(halo_sem[pair], halo.at[pair])
-        ends = [halo[pair, side].astype(jnp.float32) for side in range(2)]
-        spread(jnp.concatenate([ends[0], q, ends[1]], axis=0))
+        spread(with_halo(pair + 1, q))
         g = gradient(reach)
         kicked(g[edge : edge + rows])
         q = base[...] + whole(dq, 0, rows)
@@ -738,17 +735,13 @@
     for r in range(ring):
         for at in range(x):
             back_q[r, at] = collect(dq, r, at).astype(jnp.bfloat16)
-            back_p[0, r, at] = collect(dp, r, at).astype(jnp.bfloat16)
     to_sources(back_q, got_q.at[:, mine], q_sem)
-    to_sources(back_p.at[0], got_p.at[0, :, mine], p_sem[0])
     g = gradient(0)
-    left_over = whole(dp, 0, rows)
-    left_over = left_over - left_over.astype(jnp.bfloat16).astype(jnp.float32)
-    put(dp, left_over - half * g)
+    put(dp, whole(dp, 0, rows) - half * g)
     for r in range(ring):
         for at in range(x):
-            back_p[1, r, at] = collect(dp, r, at).astype(jnp.bfloat16)
-    to_sources(back_p.at[1], got_p.at[1, :, mine], p_sem[1])
+            back_p[r, at] = collect(dp, r, at).astype(jnp.bfloat16)
+    to_sources(back_p, got_p.at[:, mine], p_sem)
 
     def untie(value, which, out, at):
         flat = value.T
@@ -759,10 +752,9 @@
     arrive(q_sem, got_q)
     for at in range(x):
         untie(got_q[at].astype(jnp.float32), 0, q_out, at)
-    arrive(p_sem[0], got_p.at[0])
-    arrive(p_sem[1], got_p.at[1])
+    arrive(p_sem, got_p)
     for at in range(x):
-        untie(got_p[0, at].astype(jnp.float32) + got_p[1, at].astype(jnp.float32), 1, p_out, at)
+        untie(got_p[at].astype(jnp.float32), 1, p_out, at)
 
     @pl.when(outer)
     def _():
@@ -772,18 +764,17 @@
             leave(across_sem[which], all_w.at[which, 0:nx])
             leave(swap_sem[which], all_w.at[which])
 
-    leave(edge_sem, edges)
     leave(drift_edge_sem, edges_d)
     left_ring(field_sem, msg0)
     left_ring(drift_sem[0], msge)
     for k in range(1, steps):
         left_ring(drift_sem[k], msgd.at[k - 1])
+    for slot in range(pairs + 1):
+        leave(halo_sem[slot], halo.at[slot])
     for pair in range(pairs):
-        leave(halo_sem[pair], halo.at[pair])
         leave(v_sem[pair], ring_v.at[pair])
     left_ring(q_sem, back_q)
-    for part in range(2):
-        left_ring(p_sem[part], back_p.at[part])
+    left_ring(p_sem, back_p)
 
 
 def fits_ring(steps, sizes, position, filter_in):
@@ -812,7 +803,7 @@
     tiles = -(-27 * ci // lane)
     flat = jax.ShapeDtypeStruct((c * x * y, z), jnp.float32)
     reach, pairs = 4, (steps - 1) // 2
-    copies = 2 * nx + 8 + steps + 2 * pairs
+    copies = 2 * nx + 7 + steps + 2 * pairs
     edge = reach * xx
     heights = [(zb + 2 * beyond) * xx for beyond in range(2 * reach)]
     vmem = pl.BlockSpec(memory_space=pltpu.VMEM)
@@ -834,27 +825,25 @@
             pltpu.VMEM((2, 9, wide, wide), bf16),
             pltpu.VMEM((2, 9, wide, wide), bf16),
             pltpu.VMEM((x, z, lane), f32),
-            pltpu.VMEM((x, z, lane), f32),
-            pltpu.VMEM((2, x, ROWS, lane), f32),
-            pltpu.VMEM((ring, 2 * x, zb, lane), bf16),
-            pltpu.VMEM((ring, 2 * x, zb, lane), bf16),
+            pltpu.VMEM((ring, x, zb, lane), bf16),
+            pltpu.VMEM((ring, x, zb, lane), bf16),
             pltpu.VMEM((steps - 1, ring, x, zb, lane), bf16),
             pltpu.VMEM((steps - 1, ring, x, zb, lane), bf16),
-            pltpu.VMEM((ny, rows + 4 * edge, lane), f32),
+            pltpu.VMEM((ny, rows, lane), f32),
             pltpu.VMEM((3, 2, rows + 4 * edge, wide), bf16),
             pltpu.VMEM((rows + 4 * edge - 2 * xx, wide), f32),
             pltpu.VMEM((rows, wide), f32),
             pltpu.VMEM((ny, rows + 2 * edge, lane), f32),
             pltpu.VMEM((ny, rows, lane), f32),
             pltpu.VMEM((ny, rows, lane), f32),
-            pltpu.VMEM((pairs, rows, wide), bf16),
-            pltpu.VMEM((pairs, 2, 2 * edge, wide), bf16),
+            pltpu.VMEM((pairs + 1, rows, wide), bf16),
+            pltpu.VMEM((pairs + 1, 2, 2 * edge, wide), bf16),
             pltpu.VMEM((pairs, rows, wide), bf16),
             pltpu.VMEM((pairs, 2, edge, wide), bf16),
             pltpu.VMEM((ring, x, zb, lane), bf16),
             pltpu.VMEM((x, z, lane), bf16),
-            pltpu.VMEM((2, ring, x, zb, lane), bf16),
-            pltpu.VMEM((2, x, z, lane), bf16),
+            pltpu.VMEM((ring, x, zb, lane), bf16),
+            pltpu.VMEM((x, z, lane), bf16),
             pltpu.VMEM((2, c * x * y, z), f32),
             pltpu.VMEM((steps, c * x * y, z), f32),
             pltpu.VMEM((2, x, ROWS, lane), f32),

time: 33.5 us -> 32.6 us (0.973)
  Pallas kernels: 31.4 us -> 30.5 us
    pallas_call x1, Pallas kernels: 31.4 us -> 30.5 us  [on_ring(): pl.pallas_call(functools.partial(ring_kernel, steps, sizes, heights), out...]
where the time goes in v5:
time: 32.6 us; the launch traced here: 32.5 us
  Pallas kernels  30.5 us (94%)
  local copies, waits for them, and re-layouts  1.31 us (4%)
  between operations  0.64 us (2%)
    pallas_call x1, Pallas kernels, on_ring(): pl.pallas_call(functools.partial(ring_kernel, steps, sizes, heights), out...  30.5 us
    unnamed x2, local copies, waits for them, and re-layouts  1.31 us

profile of v5, /device:TPU:0, one launch (start us, length us, event | category | flops | bytes accessed | tf_op | source)
XLA Modules:
  0.0 32.5 jit_solution(5599128347478338409)
XLA Ops:
  0.6 30.5 %shard_map.77 = (f32[256,128]{1,0:T(8,128)S(1)}, f32[256,128]{1,0:T(8,128)S(1)}) custom-call(f32[256,128]{1,0:T(8,128)} %bitcast.15, f32[256,128]{1,0:T(8,128)} %bitcast.16, bf16[768,128]{1,0:T(8,128)(2,1)} %bitcast.14, bf16[27,16,32]{2,1,0:T(8,128)(2,1)} %bitcast.17, bf16[27,16,32]{2,1,0:T(8,128)(2,1)} %bitcast.18, f32[1,64]{1,0:T(1,128)} %bitcast.19), custom_call_target="tpu_custom_call" | custom-call | tf_op jit(solution)/shard_map/pallas_call | solution.py:811
  31.1 0.7 %copy.10 = f32[64,2,2,128]{3,2,1,0:T(2,128)} copy(f32[64,2,2,128]{3,2,1,0:T(2,128)S(1)} %bitcast.13) | data formatting | bytes 262144
  31.8 0.7 %copy.11 = f32[64,2,2,128]{3,2,1,0:T(2,128)} copy(f32[64,2,2,128]{3,2,1,0:T(2,128)S(1)} %bitcast.12) | data formatting | bytes 262144

commit v6 on v5

--- a/solution.py
+++ b/solution.py
@@ -299,12 +299,13 @@
     y = lane // c
     xx, yy = x * nx, y * ny
     per = lane // ci
-    tiles = own_w.shape[1]
+    half_tiles = own_w.shape[2]
     wide = yy * c
     reach = 4
     rows = zb * xx
 
     ix, iy, iz = lax.axis_index("gx"), lax.axis_index("gy"), lax.axis_index("gz")
+    ig = lax.axis_index("grp")
     me = iy * nx + ix + (iy % 2) * (nx - 1 - 2 * ix)
     block = nz * me + iz
     home = block // ring == iz
@@ -328,6 +329,11 @@
                         device_id_type=MESH,
                     )
 
+    across = [{"gy": 1 - iy}, {"grp": 1 - ig}, {"grp": 1 - ig, "gy": 1 - iy}]
+    for where in across[1:]:
+        everyone += 1
+        pl.semaphore_signal(barrier, inc=1, device_id=where, device_id_type=MESH)
+
     loads = []
     held = (pos_ref, mom_ref, noise_ref, fin_ref, fout_ref, bias_ref)
     for number in (3, 4, 0, 1, 2, 5):
@@ -345,7 +351,6 @@
             device_id_type=MESH,
         )
 
-    across = {"gy": (iy + 1) % ny}
     other = {"gz": (iz + 1) % nz}
 
     def start(source, target, number, where):
@@ -389,12 +394,12 @@
             leave(number, buf)
 
     column_sems = [[which * (nx - 1) + dx for dx in range(nx - 1)] for which in range(2)]
-    across_sem = [2 * (nx - 1), 2 * (nx - 1) + 1]
-    swap_sem = [2 * nx, 2 * nx + 1]
-    field_sem = 2 * nx + 2
-    drift_sem = [2 * nx + 3 + k for k in range(steps)]
+    across_sems = [[2 * (nx - 1) + 3 * which + i for i in range(3)] for which in range(2)]
+    swap_sem = [2 * nx + 4, 2 * nx + 5]
+    field_sem = 2 * nx + 6
+    drift_sem = [field_sem + 1 + k for k in range(steps)]
     pairs = (steps - 1) // 2
-    q_sem = 2 * nx + 3 + steps
+    q_sem = field_sem + 1 + steps
     p_sem, drift_edge_sem = q_sem + 1, q_sem + 2
     halo_sem = [q_sem + 3 + k for k in range(pairs + 1)]
     v_sem = [q_sem + 4 + pairs + k for k in range(pairs)]
@@ -406,11 +411,11 @@
     @pl.when(outer)
     def _():
         for which, ref in enumerate((fin_ref, fout_ref)):
-            for tile in range(tiles):
+            for tile in range(2 * half_tiles):
                 span = range(tile * per, min(taps, (tile + 1) * per))
                 parts = [ref[t].astype(jnp.float32) for t in span]
                 parts += [jnp.zeros((co, ci), jnp.float32)] * (per - len(parts))
-                own_w[which, tile] = jnp.concatenate(parts, axis=1).astype(jnp.bfloat16)
+                own_w[which, tile // half_tiles, tile % half_tiles] = jnp.concatenate(parts, axis=1).astype(jnp.bfloat16)
 
     def turn(ref, at):
         parts = [ref[pl.ds(at * y + j, c, stride=x * y), :] for j in range(y)]
@@ -430,24 +435,34 @@
     def to_column(which):
         for dx in range(1, nx):
             there = {"gx": (ix + dx) % nx}
-            start(own_w.at[which], all_w.at[which, me], column_sems[which][dx - 1], there)
-        start(own_w.at[which], all_w.at[which, me], across_sem[which], across)
+            start(own_w.at[which, ig], all_w.at[which, me, ig], column_sems[which][dx - 1], there)
+        for where, number in zip(across, across_sems[which]):
+            start(own_w.at[which, ig], all_w.at[which, me, ig], number, where)
+
+    def hand_over(which, gy, part):
+        piece = all_w.at[which, pl.ds(gy * nx, nx), part]
+        start(piece, piece, swap_sem[which], other)
 
     def pass_on(which):
         for dx in range(1, nx):
-            arrive(column_sems[which][dx - 1], own_w.at[which])
+            arrive(column_sems[which][dx - 1], own_w.at[which, 0])
             gx = (ix + nx - dx) % nx
-            r = iy * nx + gx + (iy % 2) * (nx - 1 - 2 * gx)
-            start(all_w.at[which, r], all_w.at[which, r], across_sem[which], across)
+            piece = all_w.at[which, iy * nx + gx + (iy % 2) * (nx - 1 - 2 * gx), ig]
+            for where, number in zip(across, across_sems[which]):
+                start(piece, piece, number, where)
+        hand_over(which, iy, ig)
+
+    def take_across(which):
+        for number, gy, part in zip(across_sems[which], (1 - iy, iy, 1 - iy), (ig, 1 - ig, 1 - ig)):
+            arrive(number, all_w.at[which, 0:nx, 0])
+            hand_over(which, gy, part)
 
     @pl.when(outer)
     def _():
         to_column(0)
-
-    @pl.when(outer)
-    def _():
         to_column(1)
-        all_w[:, me] = own_w[...]
+        for which in range(2):
+            all_w[which, me, ig] = own_w[which, ig]
 
     upper = lax.broadcasted_iota(jnp.int32, (ROWS, lane), 0) < reach
 
@@ -502,6 +517,7 @@
     @pl.when(outer)
     def _():
         pass_on(0)
+        pass_on(1)
 
     arrive(drift_edge_sem, edges_d)
     for r in range(ring):
@@ -512,14 +528,9 @@
         msge[r, x] = jnp.concatenate(beyond, axis=0).astype(jnp.bfloat16)
     send_drift(0)
 
-    def swap(which):
-        arrive(across_sem[which], all_w.at[which, 0:nx])
-        start(all_w.at[which], all_w.at[which], swap_sem[which], other)
-
     @pl.when(outer)
     def _():
-        swap(0)
-        pass_on(1)
+        take_across(0)
 
     def swapped(which):
         @pl.when(jnp.logical_not(outer))
@@ -537,11 +548,12 @@
                     for b in range(3):
                         t = a * 9 + b * 3 + cz
                         tile, spot = t // per, t % per
+                        held_at = tile // half_tiles, tile % half_tiles
                         for side in range(2):
                             pieces = []
                             for gy in range(ny):
                                 r = gy * nx + gx + (gy % 2) * (nx - 1 - 2 * gx)
-                                piece = all_w[which, r, tile].astype(jnp.float32)
+                                piece = all_w[which, r, held_at[0], held_at[1]].astype(jnp.float32)
                                 shift = (side * ny + gy - spot) % per
                                 pieces.append(pltpu.roll(piece, shift * ci, 1) if shift else piece)
                             moved[b, side] = pieces
@@ -596,7 +608,8 @@
         for at in range(x):
             scatter(stage, 0, got0[r, at].astype(jnp.float32), r, at)
     send_halo(0, whole(stage, 0, rows))
-    send_drift(1)
+    for later in range(1, steps):
+        send_drift(later)
     swapped(0)
     build(0)
     turn_over(0)
@@ -664,11 +677,9 @@
     def second_filters():
         @pl.when(outer)
         def _():
-            swap(1)
+            take_across(1)
 
         swapped(1)
-        for later in range(2, steps):
-            send_drift(later)
         build(1)
 
     def collect(ref, r, at):
@@ -760,8 +771,9 @@
     def _():
         for which in range(2):
             for number in column_sems[which]:
-                leave(number, own_w.at[which])
-            leave(across_sem[which], all_w.at[which, 0:nx])
+                leave(number, own_w.at[which, 0])
+            for number in across_sems[which]:
+                leave(number, all_w.at[which, 0:nx, 0])
             leave(swap_sem[which], all_w.at[which])
 
     leave(drift_edge_sem, edges_d)
@@ -800,10 +812,10 @@
     wide = yy * c
     rows = zb * xx
     lane = LANES
-    tiles = -(-27 * ci // lane)
+    half_tiles = -(-27 * ci // (2 * lane))
     flat = jax.ShapeDtypeStruct((c * x * y, z), jnp.float32)
     reach, pairs = 4, (steps - 1) // 2
-    copies = 2 * nx + 7 + steps + 2 * pairs
+    copies = 2 * nx + 11 + steps + 2 * pairs
     edge = reach * xx
     heights = [(zb + 2 * beyond) * xx for beyond in range(2 * reach)]
     vmem = pl.BlockSpec(memory_space=pltpu.VMEM)
@@ -820,8 +832,8 @@
             pltpu.VMEM((27, co, ci), bf16),
             pltpu.VMEM((27, co, ci), bf16),
             pltpu.VMEM((1, c), f32),
-            pltpu.VMEM((2, tiles, co, lane), bf16),
-            pltpu.VMEM((2, ring, tiles, co, lane), bf16),
+            pltpu.VMEM((2, 2, half_tiles, co, lane), bf16),
+            pltpu.VMEM((2, ring, 2, half_tiles, co, lane), bf16),
             pltpu.VMEM((2, 9, wide, wide), bf16),
             pltpu.VMEM((2, 9, wide, wide), bf16),
             pltpu.VMEM((x, z, lane), f32),
@@ -872,8 +884,8 @@
     return q.reshape(position.shape), p.reshape(momentum.shape)
 
 
-def on_device(sizes, position, momentum, noise, filter_in, filter_out, bias):
-    if fits_ring(noise.shape[0], sizes, position, filter_in):
+def on_device(groups, sizes, position, momentum, noise, filter_in, filter_out, bias):
+    if groups == 2 and fits_ring(noise.shape[0], sizes, position, filter_in):
         return on_ring(sizes, position, momentum, noise, filter_in, filter_out, bias)
     nx, ny, nz = sizes
     c, x, y, z = position.shape
@@ -938,8 +950,9 @@
     field = P(None, ("grp", "gx"), "gy", "gz")
     filters = P("gx", "gy", None, None, None)
     sizes = tuple(mesh.shape[name] for name in ("gx", "gy", "gz"))
+    groups = mesh.shape["grp"]
     return jax.shard_map(
-        functools.partial(on_device, sizes),
+        functools.partial(on_device, groups, sizes),
         mesh=mesh,
         in_specs=(field, field, P(None, None, ("grp", "gx"), "gy", "gz"), filters, filters, P()),
         out_specs=(field, field),

time: 32.6 us -> 30.9 us (0.948)
  Pallas kernels: 30.5 us -> 28.8 us
    pallas_call x1, Pallas kernels: 30.5 us -> 28.8 us  [on_ring(): pl.pallas_call(functools.partial(ring_kernel, steps, sizes, heights), out...]
where the time goes in v6:
time: 30.9 us; the launch traced here: 30.7 us
  Pallas kernels  28.8 us (93%)
  local copies, waits for them, and re-layouts  1.31 us (4%)
  between operations  0.64 us (2%)
    pallas_call x1, Pallas kernels, on_ring(): pl.pallas_call(functools.partial(ring_kernel, steps, sizes, heights), out...  28.8 us
    unnamed x2, local copies, waits for them, and re-layouts  1.31 us

profile of v6, /device:TPU:0, one launch (start us, length us, event | category | flops | bytes accessed | tf_op | source)
XLA Modules:
  0.0 30.7 jit_solution(3938236019715212545)
XLA Ops:
  0.6 28.8 %shard_map.77 = (f32[256,128]{1,0:T(8,128)S(1)}, f32[256,128]{1,0:T(8,128)S(1)}) custom-call(f32[256,128]{1,0:T(8,128)} %bitcast.15, f32[256,128]{1,0:T(8,128)} %bitcast.16, bf16[768,128]{1,0:T(8,128)(2,1)} %bitcast.14, bf16[27,16,32]{2,1,0:T(8,128)(2,1)} %bitcast.17, bf16[27,16,32]{2,1,0:T(8,128)(2,1)} %bitcast.18, f32[1,64]{1,0:T(1,128)} %bitcast.19), custom_call_target="tpu_custom_call" | custom-call | tf_op jit(solution)/shard_map/pallas_call | solution.py:823
  29.4 0.7 %copy.10 = f32[64,2,2,128]{3,2,1,0:T(2,128)} copy(f32[64,2,2,128]{3,2,1,0:T(2,128)S(1)} %bitcast.13) | data formatting | bytes 262144
  30.1 0.7 %copy.11 = f32[64,2,2,128]{3,2,1,0:T(2,128)} copy(f32[64,2,2,128]{3,2,1,0:T(2,128)S(1)} %bitcast.12) | data formatting | bytes 262144

commit v7 on v6

--- a/solution.py
+++ b/solution.py
@@ -405,30 +405,24 @@
     v_sem = [q_sem + 4 + pairs + k for k in range(pairs)]
 
     outer = iz == nz - 1
+
+    def pack(which, ref):
+        for tile in range(2 * half_tiles):
+            span = range(tile * per, min(taps, (tile + 1) * per))
+            parts = [ref[t].astype(jnp.float32) for t in span]
+            parts += [jnp.zeros((co, ci), jnp.float32)] * (per - len(parts))
+            row = jnp.concatenate(parts, axis=1).astype(jnp.bfloat16)
+            own_w[which, tile // half_tiles, tile % half_tiles] = row
+
     loads[0].wait()
-    loads[1].wait()
 
     @pl.when(outer)
     def _():
-        for which, ref in enumerate((fin_ref, fout_ref)):
-            for tile in range(2 * half_tiles):
-                span = range(tile * per, min(taps, (tile + 1) * per))
-                parts = [ref[t].astype(jnp.float32) for t in span]
-                parts += [jnp.zeros((co, ci), jnp.float32)] * (per - len(parts))
-                own_w[which, tile // half_tiles, tile % half_tiles] = jnp.concatenate(parts, axis=1).astype(jnp.bfloat16)
+        pack(0, fin_ref)
 
     def turn(ref, at):
         parts = [ref[pl.ds(at * y + j, c, stride=x * y), :] for j in range(y)]
         return jnp.concatenate(parts, axis=0).T
-
-    loads[2].wait()
-    for at in range(x):
-        flat = turn(pos_ref, at).astype(jnp.bfloat16)
-        for r in range(ring):
-            msg0[r, at] = flat[r * zb : (r + 1) * zb]
-
-    for each in sums:
-        pltpu.matmul_pop(each)
 
     pl.semaphore_wait(barrier, everyone)
 
@@ -460,6 +454,12 @@
     @pl.when(outer)
     def _():
         to_column(0)
+
+    loads[1].wait()
+
+    @pl.when(outer)
+    def _():
+        pack(1, fout_ref)
         to_column(1)
         for which in range(2):
             all_w[which, me, ig] = own_w[which, ig]
@@ -471,7 +471,14 @@
         after = ref[at, (r + 1) * zb : (r + 1) * zb + ROWS] if r < ring - 1 else beyond[1, at]
         return before, after
 
+    loads[2].wait()
+    for at in range(x):
+        flat = turn(pos_ref, at).astype(jnp.bfloat16)
+        for r in range(ring):
+            msg0[r, at] = flat[r * zb : (r + 1) * zb]
     to_owners(msg0, got0.at[me], field_sem)
+    for each in sums:
+        pltpu.matmul_pop(each)
 
     half = 0.125
     decay = float(np.exp(np.float32(-0.25)))
@@ -526,11 +533,6 @@
             before, after = around(turned_d, edges_d, r, at)
             beyond.append(jnp.where(upper, after, before))
         msge[r, x] = jnp.concatenate(beyond, axis=0).astype(jnp.bfloat16)
-    send_drift(0)
-
-    @pl.when(outer)
-    def _():
-        take_across(0)
 
     def swapped(which):
         @pl.when(jnp.logical_not(outer))
@@ -553,13 +555,13 @@
                             pieces = []
                             for gy in range(ny):
                                 r = gy * nx + gx + (gy % 2) * (nx - 1 - 2 * gx)
-                                piece = all_w[which, r, held_at[0], held_at[1]].astype(jnp.float32)
+                                piece = all_w[which, r, held_at[0], held_at[1]]
                                 shift = (side * ny + gy - spot) % per
                                 pieces.append(pltpu.roll(piece, shift * ci, 1) if shift else piece)
                             moved[b, side] = pieces
                     pairs = []
                     for b in range(yy):
-                        value = jnp.zeros((co, lane), jnp.float32)
+                        value = jnp.zeros((co, lane), jnp.bfloat16)
                         for side in range(y):
                             near = (b + side) % yy
                             if near > 2:
@@ -568,7 +570,7 @@
                                 spot = (side * ny + gy) * ci
                                 inside = (at_lane >= spot) & (at_lane < spot + ci)
                                 value = jnp.where(inside, moved[near, side][gy], value)
-                        pairs.append(value.astype(jnp.bfloat16))
+                        pairs.append(value)
                     for yo in range(yy):
                         for h in range(yy // y):
                             mats[which, a * 3 + cz, pl.ds(yo * c + row, co), h * lane : (h + 1) * lane] = (
@@ -608,11 +610,16 @@
         for at in range(x):
             scatter(stage, 0, got0[r, at].astype(jnp.float32), r, at)
     send_halo(0, whole(stage, 0, rows))
+    send_drift(0)
+
+    @pl.when(outer)
+    def _():
+        take_across(0)
+
+    swapped(0)
     for later in range(1, steps):
         send_drift(later)
-    swapped(0)
     build(0)
-    turn_over(0)
 
     def spread(value):
         n = value.shape[0]
@@ -628,8 +635,8 @@
         low, high = split_rows(height)
         sums = [[banks[unit, low, 0], banks[unit, high, int(low == high)]] for unit in range(2)]
         plans = (
-            [(0, True, True), (1, True, True), (2, True, True), (3, True, True), (4, True, False)],
-            [(8, True, True), (7, True, True), (6, True, True), (5, True, True), (4, False, True)],
+            [(3, True, True), (0, True, True), (1, True, True), (2, True, True), (4, True, False)],
+            [(5, True, True), (8, True, True), (7, True, True), (6, True, True), (4, False, True)],
         )
         for at in range(5):
             for unit in range(2):
@@ -657,11 +664,16 @@
 
     def gradient(extent, between=lambda: None, flip=False):
         n = [rows + 2 * (extent + 3 - i) * xx for i in range(4)]
-        t = jnp.tanh(conv(n[0], 0, False) + row)
+        t = jnp.tanh(conv(n[0], 0, False, flip) + row)
+        if flip:
+            turn_over(0)
         t_ref[0 : n[0]] = t
         spread(t)
         between()
-        spread(conv(n[1], 1, False, flip))
+        out = conv(n[1], 1, False, flip)
+        if flip:
+            turn_over(1)
+        spread(out)
         gu = conv(n[2], 1, True)
         t = t_ref[2 * xx : 2 * xx + n[2]]
         spread(gu * (1.0 - t * t))
@@ -675,10 +687,6 @@
         base[...] = base[...] + whole(extra, 0, rows)
 
     def second_filters():
-        @pl.when(outer)
-        def _():
-            take_across(1)
-
         swapped(1)
         build(1)
 
@@ -689,6 +697,10 @@
     def put(ref, value):
         for gy in range(ny):
             ref[gy] = value[:, gy * lane : (gy + 1) * lane]
+
+    @pl.when(outer)
+    def _():
+        take_across(1)
 
     base[...] = whole(stage, 0, rows)
     spread(with_halo(0, base[...]))
@@ -718,13 +730,11 @@
         put(dq, shift + push * now)
 
     for pair in range(pairs):
-        kicked(gradient(0, flip=pair == 0))
+        kicked(gradient(0))
         k = 2 * pair + 2
         take_drift(k - 1)
         q = base[...] + whole(dq, 0, rows)
         send_halo(pair + 1, q)
-        if pair == 0:
-            turn_over(1)
         take_drift(k)
         shift = whole(dq, 0, rows)
         v = base[...] + shift + push * (decay * whole(dp, 0, rows) - (2 * half) * shift)
@@ -743,11 +753,14 @@
         spread(jnp.concatenate([ends[0], q, ends[1]], axis=0))
 
     put(dp, decay * whole(dp, 0, rows) - half * whole(dq, 0, rows))
-    for r in range(ring):
-        for at in range(x):
-            back_q[r, at] = collect(dq, r, at).astype(jnp.bfloat16)
-    to_sources(back_q, got_q.at[:, mine], q_sem)
-    g = gradient(0)
+
+    def return_q():
+        for r in range(ring):
+            for at in range(x):
+                back_q[r, at] = collect(dq, r, at).astype(jnp.bfloat16)
+        to_sources(back_q, got_q.at[:, mine], q_sem)
+
+    g = gradient(0, return_q)
     put(dp, whole(dp, 0, rows) - half * g)
     for r in range(ring):
         for at in range(x):

time: 30.9 us -> 30.4 us (0.984)
  Pallas kernels: 28.8 us -> 28.2 us
    pallas_call x1, Pallas kernels: 28.8 us -> 28.2 us  [on_ring(): pl.pallas_call(functools.partial(ring_kernel, steps, sizes, heights), out...]
where the time goes in v7:
time: 30.4 us; the launch traced here: 30.1 us
  Pallas kernels  28.2 us (93%)
  local copies, waits for them, and re-layouts  1.31 us (4%)
  between operations  0.64 us (2%)
    pallas_call x1, Pallas kernels, on_ring(): pl.pallas_call(functools.partial(ring_kernel, steps, sizes, heights), out...  28.2 us
    unnamed x2, local copies, waits for them, and re-layouts  1.31 us

profile of v7, /device:TPU:0, one launch (start us, length us, event | category | flops | bytes accessed | tf_op | source)
XLA Modules:
  0.0 30.1 jit_solution(5499661550209231703)
XLA Ops:
  0.6 28.2 %shard_map.77 = (f32[256,128]{1,0:T(8,128)S(1)}, f32[256,128]{1,0:T(8,128)S(1)}) custom-call(f32[256,128]{1,0:T(8,128)} %bitcast.15, f32[256,128]{1,0:T(8,128)} %bitcast.16, bf16[768,128]{1,0:T(8,128)(2,1)} %bitcast.14, bf16[27,16,32]{2,1,0:T(8,128)(2,1)} %bitcast.17, bf16[27,16,32]{2,1,0:T(8,128)(2,1)} %bitcast.18, f32[1,64]{1,0:T(1,128)} %bitcast.19), custom_call_target="tpu_custom_call" | custom-call | tf_op jit(solution)/shard_map/pallas_call | solution.py:836
  28.8 0.7 %copy.10 = f32[64,2,2,128]{3,2,1,0:T(2,128)} copy(f32[64,2,2,128]{3,2,1,0:T(2,128)S(1)} %bitcast.13) | data formatting | bytes 262144
  29.5 0.7 %copy.11 = f32[64,2,2,128]{3,2,1,0:T(2,128)} copy(f32[64,2,2,128]{3,2,1,0:T(2,128)S(1)} %bitcast.12) | data formatting | bytes 262144

commit v8 on v7

--- a/solution.py
+++ b/solution.py
@@ -378,8 +378,10 @@
             go = start if j < ring else start_or_keep
             go(buf.at[at], target, number, device(owner // nz, owner % nz))
 
+    turns = sorted(range(1, ring), key=lambda j: (abs(j - ring // 2), j)) + [ring]
+
     def to_sources(buf, target, number):
-        for j in range(1, ring + 1):
+        for j in turns:
             r = (me + j) % ring
             go = start if j < ring else start_or_keep
             go(buf.at[r], target, number, device(r, block // ring))
@@ -800,6 +802,17 @@
         leave(v_sem[pair], ring_v.at[pair])
     left_ring(q_sem, back_q)
     left_ring(p_sem, back_p)
+
+
+def copy_out(q_ref, p_ref, q_out, p_out, sems):
+    copies = [
+        pltpu.make_async_copy(q_ref, q_out, sems.at[0]),
+        pltpu.make_async_copy(p_ref, p_out, sems.at[1]),
+    ]
+    for copy in copies:
+        copy.start()
+    for copy in copies:
+        copy.wait()
 
 
 def fits_ring(steps, sizes, position, filter_in):
@@ -894,6 +907,14 @@
             )
         )
     )
+    q, p = pl.pallas_call(
+        copy_out,
+        out_shape=(flat, flat),
+        in_specs=[pl.BlockSpec(memory_space=pl.ANY)] * 2,
+        out_specs=[pl.BlockSpec(memory_space=pl.ANY)] * 2,
+        scratch_shapes=[pltpu.SemaphoreType.DMA((2,))],
+        compiler_params=pltpu.CompilerParams(vmem_limit_bytes=2**20),
+    )(q, p)
     return q.reshape(position.shape), p.reshape(momentum.shape)
 
 

time: 30.4 us -> 29.6 us (0.974)
  local copies, waits for them, and re-layouts: 1.31 us -> 0 us
  Pallas kernels: 28.2 us -> 28.9 us
    unnamed x2 -> x0, local copies, waits for them, and re-layouts: 1.31 us -> none
    pallas_call x0 -> x1, Pallas kernels: none -> 0.72 us  [on_ring(): pl.pallas_call(copy_out, out_shape=(flat, flat), in_specs=[pl.BlockSpec(m...]
where the time goes in v8:
time: 29.6 us; the launch traced here: 29.5 us
  Pallas kernels  28.9 us (98%)
  between operations  0.64 us (2%)
    pallas_call x1, Pallas kernels, on_ring(): pl.pallas_call(functools.partial(ring_kernel, steps, sizes, heights), out...  28.1 us
    pallas_call x1, Pallas kernels, on_ring(): pl.pallas_call(copy_out, out_shape=(flat, flat), in_specs=[pl.BlockSpec(m...  0.72 us

profile of v8, /device:TPU:0, one launch (start us, length us, event | category | flops | bytes accessed | tf_op | source)
XLA Modules:
  0.0 29.5 jit_solution(6155118615984422739)
XLA Ops:
  0.6 28.1 %shard_map.77 = (f32[256,128]{1,0:T(8,128)S(1)}, f32[256,128]{1,0:T(8,128)S(1)}) custom-call(f32[256,128]{1,0:T(8,128)} %bitcast.13, f32[256,128]{1,0:T(8,128)} %bitcast.14, bf16[768,128]{1,0:T(8,128)(2,1)} %bitcast.12, bf16[27,16,32]{2,1,0:T(8,128)(2,1)} %bitcast.15, bf16[27,16,32]{2,1,0:T(8,128)(2,1)} %bitcast.16, f32[1,64]{1,0:T(1,128)} %bitcast.17), custom_call_target="tpu_custom_call" | custom-call | tf_op jit(solution)/shard_map/pallas_call | solution.py:849
  28.8 0.7 %shard_map.78 = (f32[256,128]{1,0:T(8,128)}, f32[256,128]{1,0:T(8,128)}) custom-call(f32[256,128]{1,0:T(8,128)S(1)} %get-tuple-element.6.q_ref, f32[256,128]{1,0:T(8,128)S(1)} %get-tuple-element.7.p_ref), custom_call_target="tpu_custom_call" | custom-call | tf_op jit(solution)/shard_map/pallas_call | solution.py:910

commit v9 on v8

--- a/solution.py
+++ b/solution.py
@@ -288,7 +288,7 @@
     inputs, refs = refs[:6], refs[6:]
     (q_out, p_out, pos_ref, mom_ref, noise_ref, fin_ref, fout_ref, bias_ref, own_w, all_w, mats,
      flipped, turned_d, msg0, got0, msgd, gotd, stage, lhs, t_ref, base, extra, dq, dp, qb,
-     halo, vb, ring_v, back_q, got_q, back_p, got_p, fixed, loose, edges_d, msge, gote, send, recv,
+     halo, vb, ring_v, back_q, got_q, back_p, got_p, fixed, loose, edges_d, msge, gote, mid, send, recv,
      load) = refs
     ring = nx * ny
     x, zb = msg0.shape[1], msg0.shape[2]
@@ -633,8 +633,11 @@
             lhs[a, 1, 0 : n - 2 * xx] = moved[xx : n - xx].astype(jnp.bfloat16)
 
     def conv(height, which, adjoint, flip=False):
+        low, high = split_rows(height)
+        return jnp.concatenate(conv_at((0, low), low, high, which, adjoint, flip), axis=0)
+
+    def conv_at(spots, low, high, which, adjoint, flip=False):
         source = mats if adjoint or flip else flipped
-        low, high = split_rows(height)
         sums = [[banks[unit, low, 0], banks[unit, high, int(low == high)]] for unit in range(2)]
         plans = (
             [(3, True, True), (0, True, True), (1, True, True), (2, True, True), (4, True, False)],
@@ -653,14 +656,15 @@
                 copy, first_row = (1, 0) if cz == 1 else (0, cz * xx)
                 fresh = at % 2
                 if use_low:
-                    left = lhs[a, copy, first_row : first_row + low]
+                    begin = first_row + spots[0]
+                    left = lhs[a, copy, begin : begin + low]
                     pltpu.matmul_acc_lhs(sums[unit][0], left, load_staged_rhs=fresh)
                     fresh = None
                 if use_high:
-                    left = lhs[a, copy, first_row + low : first_row + low + high]
+                    begin = first_row + spots[1]
+                    left = lhs[a, copy, begin : begin + high]
                     pltpu.matmul_acc_lhs(sums[unit][1], left, load_staged_rhs=fresh)
-        halves = [pltpu.matmul_pop(sums[0][part]) + pltpu.matmul_pop(sums[1][part]) for part in range(2)]
-        return jnp.concatenate(halves, axis=0)
+        return [pltpu.matmul_pop(sums[0][part]) + pltpu.matmul_pop(sums[1][part]) for part in range(2)]
 
     row = jnp.concatenate([bias_ref[...]] * yy, axis=1)
 
@@ -681,6 +685,48 @@
         spread(gu * (1.0 - t * t))
         return conv(n[3], 0, True)
 
+    def inner(q):
+        n = [rows - 2 * (i + 1) * xx for i in range(4)]
+        spread(q)
+        t = jnp.tanh(conv(n[0], 0, False) + row)
+        mid[0, 0 : n[0]] = t
+        spread(t)
+        out = conv(n[1], 1, False)
+        mid[1, 0 : n[1]] = out
+        spread(out)
+        gu = conv(n[2], 1, True)
+        t = t[2 * xx : 2 * xx + n[2]]
+        out = gu * (1.0 - t * t)
+        mid[2, 0 : n[2]] = out
+        spread(out)
+        mid[3, 0 : n[3]] = conv(n[3], 0, True)
+
+    def outside(slot, q):
+        n = [rows - 2 * (i + 1) * xx for i in range(4)]
+        side = 2 * edge
+        two = 2 * xx
+
+        def both(which, adjoint):
+            return conv_at((0, side + two), side, side, which, adjoint)
+
+        arrive(halo_sem[slot], halo.at[slot])
+        ends = [halo[slot, at].astype(jnp.float32) for at in range(2)]
+        spread(jnp.concatenate([ends[0], q[0:two], q[rows - two :], ends[1]], axis=0))
+        ends = [jnp.tanh(each + row) for each in both(0, False)]
+        t = [
+            jnp.concatenate([ends[0], mid[0, 0:two]], axis=0),
+            jnp.concatenate([mid[0, n[0] - two : n[0]], ends[1]], axis=0),
+        ]
+        spread(jnp.concatenate(t, axis=0))
+        ends = both(1, False)
+        spread(jnp.concatenate([ends[0], mid[1, 0:two], mid[1, n[1] - two : n[1]], ends[1]], axis=0))
+        gu = both(1, True)
+        near = t[0][two:], t[1][0:side]
+        ends = [each * (1.0 - at * at) for each, at in zip(gu, near)]
+        spread(jnp.concatenate([ends[0], mid[2, 0:two], mid[2, n[2] - two : n[2]], ends[1]], axis=0))
+        ends = both(0, True)
+        return jnp.concatenate([ends[0], mid[3, 0 : n[3]], ends[1]], axis=0)
+
     def take_drift(k):
         arrive(drift_sem[k], gotd.at[k - 1])
         for r in range(ring):
@@ -743,8 +789,8 @@
         vb[pair] = v.astype(jnp.bfloat16)
         start(vb.at[pair, rows - edge : rows], ring_v.at[pair, 0], v_sem[pair], right)
         start(vb.at[pair, 0:edge], ring_v.at[pair, 1], v_sem[pair], left)
-        spread(with_halo(pair + 1, q))
-        g = gradient(reach)
+        inner(q)
+        g = outside(pair + 1, q)
         kicked(g[edge : edge + rows])
         q = base[...] + whole(dq, 0, rows)
         arrive(v_sem[pair], ring_v.at[pair])
@@ -843,7 +889,7 @@
     reach, pairs = 4, (steps - 1) // 2
     copies = 2 * nx + 11 + steps + 2 * pairs
     edge = reach * xx
-    heights = [(zb + 2 * beyond) * xx for beyond in range(2 * reach)]
+    heights = [(zb + 2 * beyond) * xx for beyond in range(-reach, 2 * reach)]
     vmem = pl.BlockSpec(memory_space=pltpu.VMEM)
     bf16, f32 = jnp.bfloat16, jnp.float32
     q, p = pl.pallas_call(
@@ -887,6 +933,7 @@
             pltpu.VMEM((2, x, ROWS, lane), f32),
             pltpu.VMEM((ring, x + 1, zb, lane), bf16),
             pltpu.VMEM((ring, x + 1, zb, lane), bf16),
+            pltpu.VMEM((4, rows - 2 * xx, wide), f32),
             pltpu.SemaphoreType.DMA((copies,)),
             pltpu.SemaphoreType.DMA((copies,)),
             pltpu.SemaphoreType.DMA((6,)),

time: 29.6 us -> 29.3 us (0.990)
  Pallas kernels: 28.9 us -> 28.5 us
    pallas_call x1, Pallas kernels: 28.1 us -> 27.8 us  [on_ring(): pl.pallas_call(functools.partial(ring_kernel, steps, sizes, heights), out...]
where the time goes in v9:
time: 29.3 us; the launch traced here: 29.1 us
  Pallas kernels  28.5 us (97%)
  between operations  0.64 us (2%)
    pallas_call x1, Pallas kernels, on_ring(): pl.pallas_call(functools.partial(ring_kernel, steps, sizes, heights), out...  27.8 us
    pallas_call x1, Pallas kernels, on_ring(): pl.pallas_call(copy_out, out_shape=(flat, flat), in_specs=[pl.BlockSpec(m...  0.72 us

profile of v9, /device:TPU:0, one launch (start us, length us, event | category | flops | bytes accessed | tf_op | source)
XLA Modules:
  0.0 29.1 jit_solution(15343601563110822658)
XLA Ops:
  0.6 27.8 %shard_map.77 = (f32[256,128]{1,0:T(8,128)S(1)}, f32[256,128]{1,0:T(8,128)S(1)}) custom-call(f32[256,128]{1,0:T(8,128)} %bitcast.13, f32[256,128]{1,0:T(8,128)} %bitcast.14, bf16[768,128]{1,0:T(8,128)(2,1)} %bitcast.12, bf16[27,16,32]{2,1,0:T(8,128)(2,1)} %bitcast.15, bf16[27,16,32]{2,1,0:T(8,128)(2,1)} %bitcast.16, f32[1,64]{1,0:T(1,128)} %bitcast.17), custom_call_target="tpu_custom_call" | custom-call | tf_op jit(solution)/shard_map/pallas_call | solution.py:895
  28.4 0.7 %shard_map.78 = (f32[256,128]{1,0:T(8,128)}, f32[256,128]{1,0:T(8,128)}) custom-call(f32[256,128]{1,0:T(8,128)S(1)} %get-tuple-element.6.q_ref, f32[256,128]{1,0:T(8,128)S(1)} %get-tuple-element.7.p_ref), custom_call_target="tpu_custom_call" | custom-call | tf_op jit(solution)/shard_map/pallas_call | solution.py:957

commit v10 on v9

--- a/solution.py
+++ b/solution.py
@@ -378,13 +378,19 @@
             go = start if j < ring else start_or_keep
             go(buf.at[at], target, number, device(owner // nz, owner % nz))
 
-    turns = sorted(range(1, ring), key=lambda j: (abs(j - ring // 2), j)) + [ring]
+    turns = [0] + sorted(range(1, ring), key=lambda r: (-ring_place(r, nx)[0], r))
 
     def to_sources(buf, target, number):
-        for j in turns:
-            r = (me + j) % ring
-            go = start if j < ring else start_or_keep
-            go(buf.at[r], target, number, device(r, block // ring))
+        for r in turns:
+            kept = jnp.logical_and(home, me == r)
+
+            @pl.when(kept)
+            def _():
+                pltpu.make_async_copy(buf.at[r], target, recv.at[number]).start()
+
+            @pl.when(jnp.logical_not(kept))
+            def _():
+                start(buf.at[r], target, number, device(r, block // ring))
 
     def left_ring(number, buf):
         @pl.when(home)
@@ -640,8 +646,8 @@
         source = mats if adjoint or flip else flipped
         sums = [[banks[unit, low, 0], banks[unit, high, int(low == high)]] for unit in range(2)]
         plans = (
-            [(3, True, True), (0, True, True), (1, True, True), (2, True, True), (4, True, False)],
-            [(5, True, True), (8, True, True), (7, True, True), (6, True, True), (4, False, True)],
+            [(4, True, False), (3, True, True), (0, True, True), (1, True, True), (2, True, True)],
+            [(4, False, True), (5, True, True), (8, True, True), (7, True, True), (6, True, True)],
         )
         for at in range(5):
             for unit in range(2):
@@ -808,7 +814,8 @@
                 back_q[r, at] = collect(dq, r, at).astype(jnp.bfloat16)
         to_sources(back_q, got_q.at[:, mine], q_sem)
 
-    g = gradient(0, return_q)
+    return_q()
+    g = gradient(0)
     put(dp, whole(dp, 0, rows) - half * g)
     for r in range(ring):
         for at in range(x):

time: 29.3 us -> 29 us (0.990)
  Pallas kernels: 28.5 us -> 28.2 us
    pallas_call x1, Pallas kernels: 27.8 us -> 27.4 us  [on_ring(): pl.pallas_call(functools.partial(ring_kernel, steps, sizes, heights), out...]
where the time goes in v10:
time: 29 us; the launch traced here: 28.8 us
  Pallas kernels  28.2 us (97%)
  between operations  0.64 us (2%)
    pallas_call x1, Pallas kernels, on_ring(): pl.pallas_call(functools.partial(ring_kernel, steps, sizes, heights), out...  27.4 us
    pallas_call x1, Pallas kernels, on_ring(): pl.pallas_call(copy_out, out_shape=(flat, flat), in_specs=[pl.BlockSpec(m...  0.72 us

profile of v10, /device:TPU:0, one launch (start us, length us, event | category | flops | bytes accessed | tf_op | source)
XLA Modules:
  0.0 28.8 jit_solution(421760503241491489)
XLA Ops:
  0.6 27.4 %shard_map.77 = (f32[256,128]{1,0:T(8,128)S(1)}, f32[256,128]{1,0:T(8,128)S(1)}) custom-call(f32[256,128]{1,0:T(8,128)} %bitcast.13, f32[256,128]{1,0:T(8,128)} %bitcast.14, bf16[768,128]{1,0:T(8,128)(2,1)} %bitcast.12, bf16[27,16,32]{2,1,0:T(8,128)(2,1)} %bitcast.15, bf16[27,16,32]{2,1,0:T(8,128)(2,1)} %bitcast.16, f32[1,64]{1,0:T(1,128)} %bitcast.17), custom_call_target="tpu_custom_call" | custom-call | tf_op jit(solution)/shard_map/pallas_call | solution.py:902
  28.1 0.7 %shard_map.78 = (f32[256,128]{1,0:T(8,128)}, f32[256,128]{1,0:T(8,128)}) custom-call(f32[256,128]{1,0:T(8,128)S(1)} %get-tuple-element.6.q_ref, f32[256,128]{1,0:T(8,128)S(1)} %get-tuple-element.7.p_ref), custom_call_target="tpu_custom_call" | custom-call | tf_op jit(solution)/shard_map/pallas_call | solution.py:964

commit v11 on v10

--- a/solution.py
+++ b/solution.py
@@ -811,7 +811,7 @@
     def return_q():
         for r in range(ring):
             for at in range(x):
-                back_q[r, at] = collect(dq, r, at).astype(jnp.bfloat16)
+                back_q[r, at] = collect(dq, r, at)
         to_sources(back_q, got_q.at[:, mine], q_sem)
 
     return_q()
@@ -819,7 +819,7 @@
     put(dp, whole(dp, 0, rows) - half * g)
     for r in range(ring):
         for at in range(x):
-            back_p[r, at] = collect(dp, r, at).astype(jnp.bfloat16)
+            back_p[r, at] = collect(dp, r, at)
     to_sources(back_p, got_p.at[:, mine], p_sem)
 
     def untie(value, which, out, at):
@@ -830,10 +830,10 @@
 
     arrive(q_sem, got_q)
     for at in range(x):
-        untie(got_q[at].astype(jnp.float32), 0, q_out, at)
+        untie(got_q[at], 0, q_out, at)
     arrive(p_sem, got_p)
     for at in range(x):
-        untie(got_p[at].astype(jnp.float32), 1, p_out, at)
+        untie(got_p[at], 1, p_out, at)
 
     @pl.when(outer)
     def _():
@@ -931,10 +931,10 @@
             pltpu.VMEM((pairs + 1, 2, 2 * edge, wide), bf16),
             pltpu.VMEM((pairs, rows, wide), bf16),
             pltpu.VMEM((pairs, 2, edge, wide), bf16),
-            pltpu.VMEM((ring, x, zb, lane), bf16),
-            pltpu.VMEM((x, z, lane), bf16),
-            pltpu.VMEM((ring, x, zb, lane), bf16),
-            pltpu.VMEM((x, z, lane), bf16),
+            pltpu.VMEM((ring, x, zb, lane), f32),
+            pltpu.VMEM((x, z, lane), f32),
+            pltpu.VMEM((ring, x, zb, lane), f32),
+            pltpu.VMEM((x, z, lane), f32),
             pltpu.VMEM((2, c * x * y, z), f32),
             pltpu.VMEM((steps, c * x * y, z), f32),
             pltpu.VMEM((2, x, ROWS, lane), f32),

time: 29 us -> 31.2 us (1.076)
  Pallas kernels: 28.2 us -> 30.3 us
    pallas_call x1, Pallas kernels: 27.4 us -> 29.6 us  [on_ring(): pl.pallas_call(functools.partial(ring_kernel, steps, sizes, heights), out...]
where the time goes in v11:
time: 31.2 us; the launch traced here: 31 us
  Pallas kernels  30.3 us (97%)
  between operations  0.64 us (2%)
    pallas_call x1, Pallas kernels, on_ring(): pl.pallas_call(functools.partial(ring_kernel, steps, sizes, heights), out...  29.6 us
    pallas_call x1, Pallas kernels, on_ring(): pl.pallas_call(copy_out, out_shape=(flat, flat), in_specs=[pl.BlockSpec(m...  0.72 us

profile of v11, /device:TPU:0, one launch (start us, length us, event | category | flops | bytes accessed | tf_op | source)
XLA Modules:
  0.0 31.0 jit_solution(10602341582962670897)
XLA Ops:
  0.6 29.6 %shard_map.77 = (f32[256,128]{1,0:T(8,128)S(1)}, f32[256,128]{1,0:T(8,128)S(1)}) custom-call(f32[256,128]{1,0:T(8,128)} %bitcast.13, f32[256,128]{1,0:T(8,128)} %bitcast.14, bf16[768,128]{1,0:T(8,128)(2,1)} %bitcast.12, bf16[27,16,32]{2,1,0:T(8,128)(2,1)} %bitcast.15, bf16[27,16,32]{2,1,0:T(8,128)(2,1)} %bitcast.16, f32[1,64]{1,0:T(1,128)} %bitcast.17), custom_call_target="tpu_custom_call" | custom-call | tf_op jit(solution)/shard_map/pallas_call | solution.py:902
  30.2 0.7 %shard_map.78 = (f32[256,128]{1,0:T(8,128)}, f32[256,128]{1,0:T(8,128)}) custom-call(f32[256,128]{1,0:T(8,128)S(1)} %get-tuple-element.6.q_ref, f32[256,128]{1,0:T(8,128)S(1)} %get-tuple-element.7.p_ref), custom_call_target="tpu_custom_call" | custom-call | tf_op jit(solution)/shard_map/pallas_call | solution.py:964
